TPU v7x, 32 devices: a whole 2x2x4 slice. The times are simulated.
32 devices in a mesh: row: 8 (over z, x), col: 2 (over core), dp: 2 (over y).
Axes of the slice: x: 2, y: 2, z: 4, core: 2. Of those that a mesh axis runs over, the one named last changes fastest.
Arguments:
- pixels: bfloat16 [2, 3, 256, 256], P('dp', None, 'row', 'col'), may hold values from -6 to 6
- cotangent: bfloat16 [2, 64, 64, 1024], P('dp', 'row', 'col'), may hold values from -6 to 6
- embed_weight: bfloat16 [48, 1024], replicated, may hold values from -0.875 to 0.875
- embed_bias: float32 [1024], replicated, may hold values from -4 to 4
- layer_norm_gain: float32 [1024], replicated, may hold values from 0.5 to 1.5
- qkv_weight: bfloat16 [1024, 2304], P('row', ('col', 'dp')), may hold values from -0.1875 to 0.1875
- out_weight: bfloat16 [768, 1024], P('row', ('col', 'dp')), may hold values from -0.21875 to 0.21875
- bias_table: float32 [12, 225], replicated, may hold values from -4 to 404
- rel_index: int32 [64, 64], replicated, may hold values from 0 to 224
- shifts: int32 [2, 2], P('dp'), may hold values from 1 to 7
Outputs:
- out_weight_grad: float32 [768, 1024], P('row', ('col', 'dp'))
- embed_weight_grad: float32 [48, 1024], replicated
- embed_bias_grad: float32 [1024], replicated
- norm_gain_grad: float32 [1024], replicated
- bias_table_grad: float32 [12, 225], replicated
Inputs may be any that keep to these rules, and one draw needn't show every extreme that they name: `rel_index`: each entry names one of the 225 columns of bias_table.
All inputs are finite; a program needn't handle non-finite values.
Results may differ from a plain program's by a relative error of at most 0.023.
Values may be sent and summed in bfloat16 or wider, within the bound.
A program may use at most 64 MiB of HBM per device.

v0:
```python
import functools

import jax
import jax.numpy as jnp
from jax import lax
from jax.experimental import pallas as pl
from jax.experimental.pallas import tpu as pltpu
from jax.sharding import PartitionSpec as P

WIN = 8
PATCH = 4


norm_epsilon = 1e-05


def from_behind(value, axis, steps):
    count = lax.axis_size(axis)
    pairs = [(source, (source + steps) % count) for source in range(count)]
    return lax.ppermute(value, axis, pairs)


def make_patches(pixel_block):
    images, channels, pixel_rows, pixel_cols = pixel_block.shape
    grid_rows = pixel_rows // PATCH
    grid_cols = pixel_cols // PATCH
    shaped = pixel_block.reshape(images, channels, grid_rows, PATCH, grid_cols, PATCH)
    return shaped.transpose(0, 2, 4, 1, 3, 5).reshape(
        images, grid_rows, grid_cols, channels * PATCH * PATCH
    )


def embed_cells(patches, embed_weight, embed_bias):
    return (jnp.dot(patches, embed_weight, preferred_element_type=jnp.float32) + embed_bias).astype(
        jnp.bfloat16
    )


def window_split(block):
    rows_all, cols_all, features = block.shape
    shaped = block.reshape(rows_all // WIN, WIN, cols_all // WIN, WIN, features)
    return shaped.transpose(0, 2, 1, 3, 4).reshape(-1, WIN * WIN, features)


def window_join(windows, rows_all, cols_all):
    features = windows.shape[-1]
    shaped = windows.reshape(rows_all // WIN, cols_all // WIN, WIN, WIN, features)
    return shaped.transpose(0, 2, 1, 3, 4).reshape(rows_all, cols_all, features)

def attend_forward(cell_windows, labels, layer_norm_gain, qkv_full, bias_full):
    window_count, cell_count, features = cell_windows.shape
    head_count = bias_full.shape[0]
    inner_width = qkv_full.shape[1] // 3
    head_size = inner_width // head_count
    score_scale = head_size ** (-0.5)
    flat_rows = cell_windows.reshape(-1, features).astype(jnp.float32)
    average = jnp.mean(flat_rows, axis=-1, keepdims=True)
    centered_input = flat_rows - average
    inverse_deviation = lax.rsqrt(
        jnp.mean(centered_input * centered_input, axis=-1, keepdims=True) + norm_epsilon
    )
    standardized_rows = centered_input * inverse_deviation
    normalized_rows = (standardized_rows * layer_norm_gain).astype(jnp.bfloat16)
    projected = jnp.dot(normalized_rows, qkv_full, preferred_element_type=jnp.float32).astype(
        jnp.bfloat16
    )
    head_shape = (window_count, cell_count, head_count, head_size)
    query_rows = projected[:, :inner_width].reshape(head_shape)
    key_vectors = projected[:, inner_width : 2 * inner_width].reshape(head_shape)
    value_rows = projected[:, 2 * inner_width :].reshape(head_shape)
    scores = (
        jnp.einsum("wmhd,wnhd->whmn", query_rows, key_vectors, preferred_element_type=jnp.float32)
        * score_scale
        + bias_full[None]
    )
    same_region = labels[:, None, :, None] == labels[:, None, None, :]
    scores = jnp.where(same_region, scores, -1e30)
    row_peak = jnp.max(scores, axis=-1, keepdims=True)
    exp_scores = jnp.exp(scores - row_peak)
    attention_weights = exp_scores / jnp.sum(exp_scores, axis=-1, keepdims=True)
    reduced_probability = attention_weights.astype(jnp.bfloat16)
    attended = jnp.einsum(
        "whmn,wnhd->wmhd", reduced_probability, value_rows, preferred_element_type=jnp.float32
    ).astype(jnp.bfloat16)
    stored_residuals = (
        standardized_rows,
        inverse_deviation,
        query_rows,
        key_vectors,
        value_rows,
        attention_weights,
        reduced_probability,
    )
    return (stored_residuals, attended.reshape(-1, inner_width))


def attend_backward(stored_residuals, d_attended, layer_norm_gain, qkv_full):
    (
        standardized_rows,
        inverse_deviation,
        query_rows,
        key_vectors,
        value_rows,
        attention_weights,
        reduced_probability,
    ) = stored_residuals
    head_shape = query_rows.shape
    score_scale = head_shape[3] ** (-0.5)
    total_row_count = standardized_rows.shape[0]
    inner_width = head_shape[2] * head_shape[3]
    d_heads = d_attended.reshape(head_shape)
    d_prob = jnp.einsum("wmhd,wnhd->whmn", d_heads, value_rows, preferred_element_type=jnp.float32)
    d_values = jnp.einsum(
        "whmn,wmhd->wnhd", reduced_probability, d_heads, preferred_element_type=jnp.float32
    ).astype(jnp.bfloat16)
    d_scores = attention_weights * (
        d_prob - jnp.sum(attention_weights * d_prob, axis=-1, keepdims=True)
    )
    table_part = jnp.sum(d_scores, axis=0)
    d_low = d_scores.astype(jnp.bfloat16)
    d_queries = (
        jnp.einsum("whmn,wnhd->wmhd", d_low, key_vectors, preferred_element_type=jnp.float32)
        * score_scale
    ).astype(jnp.bfloat16)
    d_keys = (
        jnp.einsum("whmn,wmhd->wnhd", d_low, query_rows, preferred_element_type=jnp.float32)
        * score_scale
    ).astype(jnp.bfloat16)
    d_projected = jnp.concatenate(
        [
            d_queries.reshape(total_row_count, inner_width),
            d_keys.reshape(total_row_count, inner_width),
            d_values.reshape(total_row_count, inner_width),
        ],
        axis=1,
    )
    normalized_gradient = lax.dot_general(
        d_projected, qkv_full, (((1,), (1,)), ((), ())), preferred_element_type=jnp.float32
    )
    gain_contribution = jnp.sum(normalized_gradient * standardized_rows, axis=0)
    scaled_rows = normalized_gradient * layer_norm_gain
    branch_gradient = inverse_deviation * (
        scaled_rows
        - jnp.mean(scaled_rows, axis=-1, keepdims=True)
        - standardized_rows * jnp.mean(scaled_rows * standardized_rows, axis=-1, keepdims=True)
    )
    return (branch_gradient.astype(jnp.bfloat16), gain_contribution, table_part)


MESH = pl.DeviceIdType.MESH
VMEM = pltpu.VMEM


def greet_everyone(sizes, row, col, dp):
    rows, cols, dps = sizes
    barrier = pltpu.get_barrier_semaphore()
    others = 0
    for r in range(rows):
        for c in range(cols):
            for d in range(dps):
                if r or c or d:
                    others += 1
                    pl.semaphore_signal(
                        barrier,
                        inc=1,
                        device_id={
                            "row": (row + r) % rows,
                            "col": (col + c) % cols,
                            "dp": (dp + d) % dps,
                        },
                        device_id_type=MESH,
                    )
    pl.semaphore_wait(barrier, others)


def gather_kernel(
    sizes, qkv_ref, out_ref, cot_ref, pix_ref,
    qkv_all, out_all, cot_r, cot_c, cot_x, pix_r, pix_c, pix_x,
    send_sem, recv_sem, own_sem, halo_send, halo_recv,
):
    rows, cols, _ = sizes
    ring = rows // 2
    row, col, dp = lax.axis_index("row"), lax.axis_index("col"), lax.axis_index("dp")
    x, z = row % 2, row // 2
    greet_everyone(sizes, row, col, dp)
    gathered = (qkv_all, out_all)
    own = (qkv_ref, out_ref)
    started = []

    def slot(array, ident):
        flag, dy, dx, dz = ident
        column = (col + flag) % 2
        which_row = ((z - dz + ring) % ring) * 2 + (x + dx) % 2
        return gathered[array].at[column * 2 + (dp + dy) % 2, which_row]

    def semaphore(array, ident):
        flag, dy, dx, dz = ident
        return recv_sem.at[array, ((flag * 2 + dy) * 2 + dx) * ring + dz]

    def send(ident, device, landing):
        for array in range(2):
            source = own[array] if ident == (0, 0, 0, 0) else slot(array, ident)
            copy = pltpu.make_async_remote_copy(
                src_ref=source,
                dst_ref=slot(array, ident),
                send_sem=send_sem.at[len(started)],
                recv_sem=semaphore(array, landing),
                device_id=device,
                device_id_type=MESH,
            )
            copy.start()
            started.append(copy)

    def arrive(ident):
        for array in range(2):
            pltpu.make_async_remote_copy(
                src_ref=slot(array, ident),
                dst_ref=slot(array, ident),
                send_sem=send_sem.at[0],
                recv_sem=semaphore(array, ident),
                device_id={"col": (col + 1) % 2},
                device_id_type=MESH,
            ).wait_recv()

    over_y = {"dp": (dp + 1) % 2}
    over_x = {"row": z * 2 + (x + 1) % 2}
    up = {"row": ((z + 1) % ring) * 2 + x}
    down = {"row": ((z + ring - 1) % ring) * 2 + x}
    over_core = {"col": (col + 1) % 2}

    def onward_up(dy, dx, dz):
        if dz + 1 < ring // 2 or (dz + 1 == ring // 2 and dy == 0):
            send((0, dy, dx, dz), up, (0, dy, dx, dz + 1))

    def onward_down(dy, dx, back):
        if back + 1 < ring // 2 or (back + 1 == ring // 2 and dy == 1):
            send((0, dy, dx, (ring - back) % ring), down, (0, dy, dx, ring - back - 1))

    def spread(dy, dx):
        onward_up(dy, dx, 0)
        onward_down(dy, dx, 0)

    send((0, 0, 0, 0), over_y, (0, 1, 0, 0))
    send((0, 0, 0, 0), over_x, (0, 0, 1, 0))
    spread(0, 0)
    send((0, 0, 0, 0), over_core, (1, 0, 0, 0))
    local = [
        pltpu.make_async_copy(own[array], slot(array, (0, 0, 0, 0)), own_sem.at[array])
        for array in range(2)
    ]
    for copy in local:
        copy.start()
    arrive((0, 1, 0, 0))
    send((0, 1, 0, 0), over_x, (0, 1, 1, 0))
    spread(1, 0)
    above = (row + rows - 1) % rows
    left = (col + cols - 1) % cols
    edge = cot_c.shape[1]
    halos = []
    for source, target, device in (
        (pix_ref, pix_r, {"row": above}),
        (pix_ref, pix_c, {"col": left}),
        (pix_ref, pix_x, {"row": above, "col": left}),
        (cot_ref, cot_r, {"row": above}),
        (cot_ref.at[:, pl.ds(0, edge)], cot_c, {"col": left}),
        (cot_ref.at[:, pl.ds(0, edge)], cot_x, {"row": above, "col": left}),
    ):
        copy = pltpu.make_async_remote_copy(
            src_ref=source,
            dst_ref=target,
            send_sem=halo_send.at[len(halos)],
            recv_sem=halo_recv.at[len(halos)],
            device_id=device,
            device_id_type=MESH,
        )
        copy.start()
        halos.append(copy)
    send((0, 1, 0, 0), over_core, (1, 1, 0, 0))
    for dy in range(2):
        arrive((0, dy, 1, 0))
        spread(dy, 1)
        send((0, dy, 1, 0), over_core, (1, dy, 1, 0))
    for step in range(1, ring // 2 + 1):
        for dx in range(2):
            for dy in range(2):
                if step < ring // 2 or dy == 0:
                    arrive((0, dy, dx, step))
                    onward_up(dy, dx, step)
                    send((0, dy, dx, step), over_core, (1, dy, dx, step))
                if step < ring // 2 or dy == 1:
                    arrive((0, dy, dx, ring - step))
                    onward_down(dy, dx, step)
                    send((0, dy, dx, ring - step), over_core, (1, dy, dx, ring - step))
    for dz in range(ring):
        for dx in range(2):
            for dy in range(2):
                arrive((1, dy, dx, dz))
    for copy in halos:
        copy.wait_recv()
    for copy in started + halos:
        copy.wait_send()
    for copy in local:
        copy.wait()


def gather_inputs(sizes, qkv_weight, out_weight, cot_block, pix_block):
    rows, cols, dps = sizes
    groups = cols * dps
    edge = (cot_block.shape[0], WIN, cot_block.shape[2])
    cot_type, pix_type = cot_block.dtype, pix_block.dtype
    shapes = [
        ((groups, rows) + qkv_weight.shape, qkv_weight.dtype),
        ((groups, rows) + out_weight.shape, out_weight.dtype),
        (cot_block.shape, cot_type),
        (edge, cot_type),
        (edge, cot_type),
        (pix_block.shape, pix_type),
        (pix_block.shape, pix_type),
        (pix_block.shape, pix_type),
    ]
    return pl.pallas_call(
        functools.partial(gather_kernel, sizes),
        out_shape=[jax.ShapeDtypeStruct(shape, kind) for shape, kind in shapes],
        in_specs=[pl.BlockSpec(memory_space=VMEM)] * 4,
        out_specs=[pl.BlockSpec(memory_space=VMEM)] * 8,
        scratch_shapes=[
            pltpu.SemaphoreType.DMA((4 * rows * groups,)),
            pltpu.SemaphoreType.DMA((2, rows * groups)),
            pltpu.SemaphoreType.DMA((2,)),
            pltpu.SemaphoreType.DMA((6,)),
            pltpu.SemaphoreType.DMA((6,)),
        ],
        compiler_params=pltpu.CompilerParams(
            collective_id=0, has_side_effects=True, vmem_limit_bytes=40 * 2**20
        ),
        name="gather_inputs",
    )(qkv_weight, out_weight, cot_block, pix_block)


def reduce_kernel(
    sizes, grad_ref, small_ref, grad_out, small_out,
    core_g, core_e, made_g, made_e, z_g, z_e, acc_g, acc_e,
    xs_g, xs_e, x_g, x_e, ys_g, y_g, ys_e, y_e, tot_e,
    core_send, core_recv, z_send, z_recv, xy_send, xy_recv, all_send, all_recv,
):
    rows, cols, dps = sizes
    ring = rows // 2
    row, col, dp = lax.axis_index("row"), lax.axis_index("col"), lax.axis_index("dp")
    x, z = row % 2, row // 2
    f32, low = jnp.float32, jnp.bfloat16
    greet_everyone(sizes, row, col, dp)
    other = (col + 1) % 2

    def remote(source, target, send_sem, recv_sem, device):
        copy = pltpu.make_async_remote_copy(
            src_ref=source, dst_ref=target, send_sem=send_sem, recv_sem=recv_sem,
            device_id=device, device_id_type=MESH,
        )
        copy.start()
        return copy

    order = [ring // 2] + [s for s in range(1, ring) if s != ring // 2] + [0]
    across = {}
    for s in order:
        there = ((z + s) % ring) * 2
        across[s] = [
            remote(
                source.at[pl.ds(other * 2, 2), pl.ds(there, 2)], target.at[s],
                core_send.at[i, s], core_recv.at[i, s], {"col": other},
            )
            for i, (source, target) in enumerate(((grad_ref, core_g), (small_ref, core_e)))
        ]
    sent = []
    for s in order:
        for copy in across[s]:
            copy.wait_recv()
        there = ((z + s) % ring) * 2
        for d in range(2):
            for h in range(2):
                total = grad_ref[col * 2 + d, there + h].astype(f32) + core_g[s, d, h].astype(f32)
                small = small_ref[col * 2 + d, there + h] + core_e[s, d, h]
                if s:
                    made_g[s, d, h] = total.astype(low)
                    made_e[s, d, h] = small
                else:
                    acc_g[d, h] = total
                    acc_e[d, h] = small
        if s:
            device = {"row": there + x}
            sent.append(remote(made_g.at[s], z_g.at[s], z_send.at[0, s], z_recv.at[0, s], device))
            sent.append(remote(made_e.at[s], z_e.at[s], z_send.at[1, s], z_recv.at[1, s], device))
    for copy in sent:
        copy.wait_recv()

    def z_sum(d, h):
        total, small = acc_g[d, h], acc_e[d, h]
        for s in range(1, ring):
            total = total + z_g[s, d, h].astype(f32)
            small = small + z_e[s, d, h]
        return total, small

    away = (x + 1) % 2
    for d in range(2):
        total, small = z_sum(d, away)
        xs_g[d] = total.astype(low)
        xs_e[d] = small
    device = {"row": z * 2 + away}
    pair = [
        remote(xs_g, x_g, xy_send.at[0], xy_recv.at[0], device),
        remote(xs_e, x_e, xy_send.at[1], xy_recv.at[1], device),
    ]
    mine, mine_small = z_sum(dp, x)
    far, far_small = z_sum((dp + 1) % 2, x)
    for copy in pair:
        copy.wait_recv()
    ys_g[...] = (far + x_g[(dp + 1) % 2].astype(f32)).astype(low)
    ys_e[...] = far_small + x_e[(dp + 1) % 2]
    device = {"dp": (dp + 1) % 2}
    last = [
        remote(ys_e, y_e, xy_send.at[3], xy_recv.at[3], device),
        remote(ys_g, y_g, xy_send.at[2], xy_recv.at[2], device),
    ]
    mine = mine + x_g[dp].astype(f32)
    mine_small = mine_small + x_e[dp]
    last[0].wait_recv()
    group = col * 2 + dp
    whole = mine_small + y_e[...]
    tot_e[...] = whole
    spread = []
    for r in range(rows):
        for c in range(cols):
            for d in range(dps):
                if r or c or d:
                    index = (r * cols + c) * dps + d
                    spread.append(
                        remote(
                            tot_e, small_out.at[group, row],
                            all_send.at[index], all_recv.at[index],
                            {
                                "row": (row + r) % rows,
                                "col": (col + c) % cols,
                                "dp": (dp + d) % dps,
                            },
                        )
                    )
    small_out[group, row] = whole
    last[1].wait_recv()
    grad_out[...] = mine + y_g[...].astype(f32)
    index = 0
    for r in range(rows):
        for c in range(cols):
            for d in range(dps):
                if r or c or d:
                    place = (r * cols + c) * dps + d
                    source_group = ((col + cols - c) % cols) * dps + (dp + dps - d) % dps
                    pltpu.make_async_remote_copy(
                        src_ref=tot_e,
                        dst_ref=small_out.at[source_group, (row + rows - r) % rows],
                        send_sem=all_send.at[place],
                        recv_sem=all_recv.at[place],
                        device_id={"col": other},
                        device_id_type=MESH,
                    ).wait_recv()
    for s in order:
        for copy in across[s]:
            copy.wait_send()
    for copy in sent + pair + last + spread:
        copy.wait_send()


def reduce_outputs(sizes, grad_blocks, small_blocks):
    rows, cols, dps = sizes
    ring = rows // 2
    big, tiny = grad_blocks.shape[2:], small_blocks.shape[2:]
    f32, low = jnp.float32, jnp.bfloat16
    dma = pltpu.SemaphoreType.DMA
    return pl.pallas_call(
        functools.partial(reduce_kernel, sizes),
        out_shape=[
            jax.ShapeDtypeStruct(big, f32),
            jax.ShapeDtypeStruct(small_blocks.shape, f32),
        ],
        in_specs=[pl.BlockSpec(memory_space=VMEM)] * 2,
        out_specs=[pl.BlockSpec(memory_space=VMEM)] * 2,
        scratch_shapes=[
            VMEM((ring, 2, 2) + big, low), VMEM((ring, 2, 2) + tiny, f32),
            VMEM((ring, 2, 2) + big, low), VMEM((ring, 2, 2) + tiny, f32),
            VMEM((ring, 2, 2) + big, low), VMEM((ring, 2, 2) + tiny, f32),
            VMEM((2, 2) + big, f32), VMEM((2, 2) + tiny, f32),
            VMEM((2,) + big, low), VMEM((2,) + tiny, f32),
            VMEM((2,) + big, low), VMEM((2,) + tiny, f32),
            VMEM(big, low), VMEM(big, low), VMEM(tiny, f32), VMEM(tiny, f32), VMEM(tiny, f32),
            dma((2, ring)), dma((2, ring)), dma((2, ring)), dma((2, ring)),
            dma((4,)), dma((4,)),
            dma((rows * cols * dps,)), dma((rows * cols * dps,)),
        ],
        compiler_params=pltpu.CompilerParams(
            collective_id=1, has_side_effects=True, vmem_limit_bytes=40 * 2**20
        ),
        name="reduce_outputs",
    )(grad_blocks, small_blocks)


def on_device(
    direct,
    sizes,
    pixels,
    cotangent,
    embed_weight,
    embed_bias,
    layer_norm_gain,
    qkv_weight,
    out_weight,
    bias_table,
    rel_index,
    shifts,
):
    images, rows_dev, cols_dev, features = cotangent.shape
    rows, cols, dps = sizes
    head_count, table_size = bias_table.shape
    pix_block, cot_block = pixels[0], cotangent[0]
    row_shift, col_shift = shifts[0, 0], shifts[0, 1]
    if direct:
        qkv_all, out_all, cot_r, cot_c, cot_x, pix_r, pix_c, pix_x = gather_inputs(
            sizes, qkv_weight, out_weight, cot_block, pix_block
        )
        qkv_full = jnp.concatenate(
            [w.reshape(-1, qkv_weight.shape[1]) for w in qkv_all], axis=1
        )
        out_full = jnp.concatenate(
            [w.reshape(-1, out_weight.shape[1]) for w in out_all], axis=1
        )
    else:
        qkv_full, out_full = [
            lax.all_gather(
                lax.all_gather(w, "row", axis=0, tiled=True), ("col", "dp"), axis=1, tiled=True
            )
            for w in (qkv_weight, out_weight)
        ]
        pix_r, cot_r = from_behind((pix_block, cot_block), "row", -1)
        pix_c, cot_c = from_behind((pix_block, cot_block[:, :WIN]), "col", -1)
        pix_x, cot_x = from_behind((pix_c, cot_c), "row", -1)
    wide_pix = jnp.concatenate(
        [
            jnp.concatenate([pix_block, pix_c[:, :, : WIN * PATCH]], axis=2),
            jnp.concatenate([pix_r, pix_x[:, :, : WIN * PATCH]], axis=2),
        ],
        axis=1,
    )
    wide_cot = jnp.concatenate(
        [
            jnp.concatenate([cot_block, cot_c], axis=1),
            jnp.concatenate([cot_r, cot_x], axis=1),
        ],
        axis=0,
    )
    wide_patches = make_patches(wide_pix[None])[0]
    patches = lax.dynamic_slice(
        wide_patches, (row_shift, col_shift, 0), (rows_dev, cols_dev, wide_patches.shape[2])
    )
    shifted_cot = lax.dynamic_slice(
        wide_cot, (row_shift, col_shift, 0), (rows_dev, cols_dev, features)
    )
    patch_rows = window_split(patches).reshape(-1, patches.shape[2])
    cot_flat = window_split(shifted_cot).reshape(-1, features)
    grid_rows, grid_cols = rows_dev * rows, cols_dev * cols
    row_ids = lax.axis_index("row") * rows_dev + jnp.arange(rows_dev, dtype=jnp.int32)
    col_ids = lax.axis_index("col") * cols_dev + jnp.arange(cols_dev, dtype=jnp.int32)
    row_part = (row_ids >= grid_rows - row_shift).astype(jnp.int32)
    col_part = (col_ids >= grid_cols - col_shift).astype(jnp.int32)
    region = 2 * row_part[:, None] + col_part[None, :]
    labels = window_split(region[:, :, None])[:, :, 0]
    selector = (
        rel_index.reshape(-1)[:, None] == jnp.arange(table_size, dtype=jnp.int32)[None, :]
    ).astype(jnp.float32)
    bias_full = jnp.dot(selector, bias_table.T, precision=lax.Precision.HIGHEST).T.reshape(
        head_count, WIN * WIN, WIN * WIN
    )
    cells = embed_cells(patch_rows, embed_weight, embed_bias)
    stored_residuals, attended = attend_forward(
        cells.reshape(-1, WIN * WIN, features), labels, layer_norm_gain, qkv_full, bias_full
    )
    d_attended = lax.dot_general(
        cot_flat, out_full, (((1,), (1,)), ((), ())), preferred_element_type=jnp.float32
    ).astype(jnp.bfloat16)
    d_rows, gain_contribution, table_part = attend_backward(
        stored_residuals, d_attended, layer_norm_gain, qkv_full
    )
    table_grad = jnp.dot(
        table_part.reshape(head_count, -1), selector, precision=lax.Precision.HIGHEST
    )
    contract = (((0,), (0,)), ((), ()))
    back_rows = jnp.concatenate([cot_flat, d_rows], axis=0)
    embed_grad = lax.dot_general(
        jnp.concatenate([patch_rows, patch_rows], axis=0),
        back_rows,
        contract,
        preferred_element_type=jnp.float32,
    )
    bias_grad = jnp.sum(back_rows, axis=0, dtype=jnp.float32)
    if not direct:
        partial_rows = lax.psum_scatter(
            lax.dot_general(attended, cot_flat, contract, preferred_element_type=jnp.float32),
            "row",
            scatter_dimension=0,
            tiled=True,
        )
        out_weight_grad = lax.psum_scatter(
            partial_rows, ("col", "dp"), scatter_dimension=1, tiled=True
        )
        totals = lax.psum(
            (embed_grad, bias_grad, gain_contribution, table_grad), ("row", "col", "dp")
        )
        return (out_weight_grad,) + totals
    groups = cols * dps
    cot_groups = cot_flat.reshape(-1, groups, features // groups)
    grad_blocks = jnp.stack(
        [
            lax.dot_general(
                attended, cot_groups[:, k], contract, preferred_element_type=jnp.float32
            ).astype(jnp.bfloat16)
            for k in range(groups)
        ]
    ).reshape((groups, rows) + out_weight.shape)
    pieces = (embed_grad, bias_grad, gain_contribution, table_grad)
    flat = jnp.concatenate([piece.reshape(-1) for piece in pieces])
    unit = groups * rows * 2048
    flat = jnp.pad(flat, (0, -flat.shape[0] % unit))
    out_weight_grad, small = reduce_outputs(
        sizes, grad_blocks, flat.reshape(groups, rows, -1, 256)
    )
    small = small.reshape(-1)
    totals, start = [], 0
    for piece in pieces:
        totals.append(small[start : start + piece.size].reshape(piece.shape))
        start += piece.size
    return (out_weight_grad,) + tuple(totals)


def solution(mesh):
    sizes = tuple(mesh.shape[name] for name in ("row", "col", "dp"))
    direct = sizes[1:] == (2, 2) and sizes[0] == 8
    return jax.shard_map(
        functools.partial(on_device, direct, sizes),
        mesh=mesh,
        in_specs=(
            P("dp", None, "row", "col"),
            P("dp", "row", "col", None),
            P(),
            P(),
            P(),
            P("row", ("col", "dp")),
            P("row", ("col", "dp")),
            P(),
            P(),
            P("dp", None),
        ),
        out_specs=(P("row", ("col", "dp")), P(), P(), P(), P()),
        check_vma=False,
    )
```

profile of v0, /device:TPU:1, one launch (start us, length us, event | category | flops | bytes accessed | tf_op | source)
XLA Modules:
  0.0 202.6 jit_solution(4224717791583351686)
XLA Ops:
  0.7 1.3 fusion.76
  7.4 0.8 eq.39
  8.3 1.1 copy.117.qkv_ref
  9.4 2.7 %convolution_bitcast_fusion = f32[12,4096]{1,0:T(8,128)S(1)} fusion(f32[12,225]{1,0:T(8,128)} %param.17, s32[4096]{0:T(1024)S(1)} %eq.39), kind=kOutput, calls=%fused_computation.1 | convolution fusion | flops 133632000 | bytes 223792 | tf_op jit(solution)/shard_map/dot_general | solution.py:576
  12.3 0.9 copy.126
  13.2 81.5 %gather_inputs.1 = (bf16[4,8,128,576]{3,2,1,0:T(8,128)(2,1)S(1)}, bf16[4,8,96,256]{3,2,1,0:T(8,128)(2,1)S(1)}, bf16[8,32,1024]{2,1,0:T(8,128)(2,1)S(1)}, bf16[8,...) custom-call(bf16[128,576]{1,0:T(8,128)(2,1)S(1)} %copy.117.qkv_ref, ...), custom_call_target="tpu_custom_call" | custom-call | tf_op jit(solution)/shard_map/gather_inputs/pallas_call | solution.py:321
  94.7 2.3 %copy-done.1 = bf16[4,8,128,576]{3,2,1,0:T(8,128)(2,1)} copy-done((bf16[4,8,128,576]{3,2,1,0:T(8,128)(2,1)}, bf16[4,8,128,576]{3,2,1,0:T(8,128)(2,1)S(1)}, u32[]{:S(2)}) %copy-start.1) | copy-done | bytes 4718616
  97.0 1.1 fusion.49
  98.5 1.8 fusion.74
  100.5 0.6 fusion.19
  101.1 0.6 reshape.158
  101.7 1.5 copy.145
  103.3 1.3 reshape_broadcast_in_dim.4
  104.6 1.6 copy.118
  106.4 0.7 copy.131
  107.8 4.6 %fusion.71 = (bf16[1,8,128,576]{3,2,1,0:T(8,128)(2,1)S(1)}, bf16[1,8,128,576]{3,2,1,0:T(8,128)(2,1)S(1)}, bf16[1,8,128,576]{3,2,1,0:T(8,128)(2,1)}, bf16[1,8,128,576]{3,2,1,0:T(8,128)(2,1)}) fusion(bf16[4,8,128,576]{3,2,1,0:T(8,128)(2,1)} %copy-done.1), kind=kLoop, calls=%fused_computation.109 | loop fusion | bytes 9437184 | tf_op jit(solution)/shard_map/unstack | solution.py:528
  112.4 8.1 %concatenate.40 = bf16[1024,2304]{1,0:T(8,128)(2,1)} concatenate(bf16[1024,576]{1,0:T(8,128)(2,1)} %bitcast.107, bf16[1024,576]{1,0:T(8,128)(2,1)} %bitcast.106, bf16[1024,576]{1,0:T(8,128)(2,1)S(1)} %bitcast.105, bf16[1024,576]{1,0:T(8,128)(2,1)S(1)} %bitcast.104), dimensions={1} | concatenate | bytes 9437184 | tf_op jit(solution)/shard_map/concatenate | solution.py:527
  120.6 3.8 %convolution_convert_fusion = bf16[256,2304]{1,0:T(8,128)(2,1)S(1)} fusion(bf16[1024,2304]{1,0:T(8,128)(2,1)} %concatenate.40, bf16[256,1024]{1,0:T(8,128)(2,1)S(1)} %get-tuple-element.50, f32[1024]{0:T(1024)S(1)} %copy-done.23, f32[256]{0:T(256)S(1)} %add_rsqrt_fusion, f32[256]{0:T(256)S(1)} %broadcast_multiply_fusion.2), kind=kOutput, calls=%fused_computation.4 | convolution fusion | flops 1209860096 | bytes 6428672 | tf_op jit(solution)/shard_map/dot_general | solution.py:64
  124.5 0.6 reshape.157
  125.1 0.9 copy.137
  126.0 1.7 reshape.155
  127.6 0.6 reshape.156
  128.3 1.1 copy.141
  129.4 0.4 add_select_fusion
  129.8 2.4 %fusion.77 = (f32[4,12,64]{2,1,0:T(8,128)S(1)}, f32[4,12,64,64]{2,3,1,0:T(8,128)S(1)}) fusion(f32[4,12,64,64]{2,3,1,0:T(8,128)S(1)} %add_select_fusion), kind=kOutput, calls=%fused_computation.115 | output fusion | flops 393279 | bytes 1585152 | tf_op jit(solution)/shard_map/sub | solution.py:79
  132.2 4.1 %fusion.16 = bf16[4,64,12,64]{1,3,2,0:T(8,128)(2,1)} fusion(bf16[4,64,12,64]{1,3,2,0:T(8,128)(2,1)} %copy.145, f32[4,12,64]{2,1,0:T(8,128)S(1)} %get-tuple-element.51, f32[4,12,64,64]{2,3,1,0:T(8,128)} %copy-done.6), kind=kOutput, calls=%fused_computation.35 | convolution fusion | flops 25955392 | bytes 1585152 | tf_op jit(solution)/shard_map/whmn,wmhd->wnhd/dot_general | solution.py:113
  136.3 3.7 %fusion.15 = bf16[4,64,12,64]{1,3,2,0:T(8,128)(2,1)} fusion(bf16[4,64,12,64]{3,2,1,0:T(8,128)(2,1)} %reshape.155, f32[4,12,64]{2,1,0:T(8,128)S(1)} %get-tuple-element.51, f32[4,12,64,64]{2,3,1,0:T(8,128)} %copy-done.6), kind=kOutput, calls=%fused_computation.34 | convolution fusion | flops 25955392 | bytes 1585152 | tf_op jit(solution)/shard_map/whmn,wnhd->wmhd/dot_general | solution.py:82
  140.1 1.9 multiply_reduce_fusion
  142.0 1.9 fusion.42
  144.3 1.4 fusion.1
  145.8 0.5 fusion.18
  146.3 0.6 fusion.17
  146.9 0.6 copy.140
  147.5 1.2 reshape.145
  148.8 0.8 copy.144
  149.6 1.3 reshape.146
  150.9 0.6 copy.129
  151.5 0.5 reshape.142
  152.1 0.6 copy.147
  152.7 0.5 reshape.147
  153.3 4.1 %fusion.35 = (f32[256]{0:T(256)S(1)}, f32[1024]{0:T(1024)S(1)}, f32[256]{0:T(256)S(1)}, f32[256,1024]{1,0:T(8,128)S(1)}) fusion(bf16[256,1024]{1,0:T(8,128)(2,1)S(1)} %copy-done.10, f32[1024]{0:T(1024)S(1)} %copy-done.24, f32[256]{0:T(256)S(1)} %copy-done.26, f32[256]{0:T(256)S(1)} %copy-done.22, bf16[1024,2304]{1,0:T(8,128)(2,1)} %concatenate.40, ...), kind=kOutput, calls=%fused_computation.57 | convolution fusion | flops 1213856256 | bytes 7483392 | tf_op jit(solution)/shard_map/dot_general | solution.py:137
  157.8 0.6 copy-done.8
  159.1 0.5 copy-done.17
  160.9 38.9 %reduce_outputs.1 = (f32[96,256]{1,0:T(8,128)S(1)}, f32[4,8,8,256]{3,2,1,0:T(8,128)S(1)}) custom-call(bf16[4,8,96,256]{3,2,1,0:T(8,128)(2,1)S(1)} %pad_maximum_fusion.grad_ref, f32[4,8,8,256]{3,2,1,0:T(8,128)S(1)} %reshape.151.small_ref), custom_call_target="tpu_custom_call" | custom-call | tf_op jit(solution)/shard_map/reduce_outputs/pallas_call | solution.py:477
  199.8 0.7 reshape.152
  200.7 0.6 fusion.75
  201.3 0.7 reshape.154
  202.0 0.6 copy.192
  (89 shorter events, 5.0 us)
Async XLA Ops:
  0.6 106.5 %copy-start = (bf16[48,1024]{1,0:T(8,128)(2,1)S(1)}, bf16[48,1024]{1,0:T(8,128)(2,1)}, u32[]{:S(2)}) copy-start(bf16[48,1024]{1,0:T(8,128)(2,1)} %param.12) | copy-start | bytes 294916
  0.6 12.5 %copy-start.4 = (bf16[96,256]{1,0:T(8,128)(2,1)S(1)}, bf16[96,256]{1,0:T(8,128)(2,1)}, u32[]{:S(2)}) copy-start(bf16[96,256]{1,0:T(8,128)(2,1)} %out_ref.1) | copy-start | bytes 147460
  0.7 12.5 %copy-start.2 = (bf16[1,8,32,1024]{3,2,1,0:T(8,128)(2,1)S(1)}, bf16[1,8,32,1024]{3,2,1,0:T(8,128)(2,1)}, u32[]{:S(2)}) copy-start(bf16[1,8,32,1024]{3,2,1,0:T(8,128)(2,1)} %param.11) | copy-start | bytes 1572868
  0.7 12.5 %copy-start.3 = (bf16[1,3,32,128]{3,2,1,0:T(8,128)(2,1)S(1)}, bf16[1,3,32,128]{3,2,1,0:T(8,128)(2,1)}, u32[]{:S(2)}) copy-start(bf16[1,3,32,128]{3,2,1,0:T(8,128)(2,1)} %param.10) | copy-start | bytes 73732
  94.7 2.3 %copy-start.1 = (bf16[4,8,128,576]{3,2,1,0:T(8,128)(2,1)}, bf16[4,8,128,576]{3,2,1,0:T(8,128)(2,1)S(1)}, u32[]{:S(2)}) copy-start(bf16[4,8,128,576]{3,2,1,0:T(8,128)(2,1)S(1)} %get-tuple-element.18) | copy-start | bytes 14155780
  98.1 2.3 %copy-start.7 = (bf16[1,4,8,8,1024]{4,3,2,1,0:T(8,128)(2,1)}, bf16[1,4,8,8,1024]{4,3,2,1,0:T(8,128)(2,1)S(1)}, u32[]{:S(2)}) copy-start(bf16[1,4,8,8,1024]{4,3,2,1,0:T(8,128)(2,1)S(1)} %copy.130) | copy-start | bytes 1572868
  104.6 2.6 %copy-start.27 = (f32[1024]{0:T(1024)S(1)}, f32[1024]{0:T(1024)}, u32[]{:S(2)}) copy-start(f32[1024]{0:T(1024)} %param.13) | copy-start | bytes 12292
  107.5 13.1 %copy-start.9 = (bf16[256,1024]{1,0:T(8,128)(2,1)}, bf16[256,1024]{1,0:T(8,128)(2,1)S(1)}, u32[]{:S(2)}) copy-start(bf16[256,1024]{1,0:T(8,128)(2,1)S(1)} %get-tuple-element.50) | copy-start | bytes 1572868
  107.5 13.1 %copy-start.21 = (f32[256]{0:T(256)}, f32[256]{0:T(256)S(1)}, u32[]{:S(2)}) copy-start(f32[256]{0:T(256)S(1)} %broadcast_multiply_fusion.2) | copy-start | bytes 3076
  107.8 12.8 %copy-start.25 = (f32[256]{0:T(256)}, f32[256]{0:T(256)S(1)}, u32[]{:S(2)}) copy-start(f32[256]{0:T(256)S(1)} %add_rsqrt_fusion) | copy-start | bytes 3076
  112.4 8.1 %copy-start.23 = (f32[1024]{0:T(1024)S(1)}, f32[1024]{0:T(1024)}, u32[]{:S(2)}) copy-start(f32[1024]{0:T(1024)} %param.14) | copy-start | bytes 12292
  127.6 1.7 copy-start.11
  129.8 2.4 %copy-start.6 = (f32[4,12,64,64]{2,3,1,0:T(8,128)}, f32[4,12,64,64]{2,3,1,0:T(8,128)S(1)}, u32[]{:S(2)}) copy-start(f32[4,12,64,64]{2,3,1,0:T(8,128)S(1)} %add_select_fusion) | copy-start | bytes 2359300
  132.2 7.9 %copy-start.5 = (f32[4,12,64,64]{2,3,1,0:T(8,128)}, f32[4,12,64,64]{2,3,1,0:T(8,128)S(1)}, u32[]{:S(2)}) copy-start(f32[4,12,64,64]{2,3,1,0:T(8,128)S(1)} %get-tuple-element.52) | copy-start | bytes 2359300
  149.6 1.3 copy-start.13
  150.9 1.1 copy-start.12
  152.0 1.2 copy-start.10
  152.0 1.2 copy-start.18
  152.0 1.3 copy-start.19
  152.1 1.3 copy-start.22
  152.1 1.3 copy-start.24
  152.1 1.2 copy-start.26
  157.4 1.0 copy-start.8
  157.4 1.2 copy-start.20
  158.6 1.0 copy-start.17
  158.9 1.0 copy-start.16
  158.9 1.2 copy-start.15
  159.0 1.4 copy-start.14
where the time goes:
time: 204 us; the launch traced here: 203 us
  Pallas kernels  120 us (59%)
  local copies, waits for them, and re-layouts  43.5 us (21%)
  matrix products  25.7 us (13%)
  other arithmetic  6.65 us (3%)
  between operations  6.44 us (3%)
    pallas_call x1, Pallas kernels, gather_inputs(): pl.pallas_call(functools.partial(gather_kernel, sizes), out_shape=[jax.Sh...  81.5 us
    pallas_call x1, Pallas kernels, reduce_outputs(): pl.pallas_call(functools.partial(reduce_kernel, sizes), out_shape=[jax.Sh...  38.9 us
    concatenate x1, local copies, waits for them, and re-layouts, on_device(): jnp.concatenate([w.reshape(-1, qkv_weight.shape[1]) for w in qkv_all], ax...  8.12 us
    unnamed x60, local copies, waits for them, and re-layouts  5.58 us
    another operation x1, local copies, waits for them, and re-layouts, on_device(): qkv_full = jnp.concatenate([w.reshape(-1, qkv_weight.shape[1]) for w in q...  4.62 us
    dot_general x1, matrix products, attend_backward(): jnp.einsum('whmn,wmhd->wnhd', reduced_probability, d_heads, preferred_ele...  4.13 us

commit v1 on v0

v1 whole, which is shorter than its diff:
```python
import functools

import jax
import jax.numpy as jnp
from jax import lax
from jax.experimental import pallas as pl
from jax.experimental.pallas import tpu as pltpu
from jax.sharding import PartitionSpec as P

WIN = 8
PATCH = 4


norm_epsilon = 1e-05


def from_behind(value, axis, steps):
    count = lax.axis_size(axis)
    pairs = [(source, (source + steps) % count) for source in range(count)]
    return lax.ppermute(value, axis, pairs)


def make_patches(pixel_block):
    images, channels, pixel_rows, pixel_cols = pixel_block.shape
    grid_rows = pixel_rows // PATCH
    grid_cols = pixel_cols // PATCH
    shaped = pixel_block.reshape(images, channels, grid_rows, PATCH, grid_cols, PATCH)
    return shaped.transpose(0, 2, 4, 1, 3, 5).reshape(
        images, grid_rows, grid_cols, channels * PATCH * PATCH
    )


def embed_cells(patches, embed_weight, embed_bias):
    return (jnp.dot(patches, embed_weight, preferred_element_type=jnp.float32) + embed_bias).astype(
        jnp.bfloat16
    )


def window_split(block):
    rows_all, cols_all, features = block.shape
    shaped = block.reshape(rows_all // WIN, WIN, cols_all // WIN, WIN, features)
    return shaped.transpose(0, 2, 1, 3, 4).reshape(-1, WIN * WIN, features)


def window_join(windows, rows_all, cols_all):
    features = windows.shape[-1]
    shaped = windows.reshape(rows_all // WIN, cols_all // WIN, WIN, WIN, features)
    return shaped.transpose(0, 2, 1, 3, 4).reshape(rows_all, cols_all, features)

def attend_forward(cell_windows, labels, layer_norm_gain, qkv_full, bias_full):
    window_count, cell_count, features = cell_windows.shape
    head_count = bias_full.shape[0]
    inner_width = qkv_full.shape[1] // 3
    head_size = inner_width // head_count
    score_scale = head_size ** (-0.5)
    flat_rows = cell_windows.reshape(-1, features).astype(jnp.float32)
    average = jnp.mean(flat_rows, axis=-1, keepdims=True)
    centered_input = flat_rows - average
    inverse_deviation = lax.rsqrt(
        jnp.mean(centered_input * centered_input, axis=-1, keepdims=True) + norm_epsilon
    )
    standardized_rows = centered_input * inverse_deviation
    normalized_rows = (standardized_rows * layer_norm_gain).astype(jnp.bfloat16)
    projected = jnp.dot(normalized_rows, qkv_full, preferred_element_type=jnp.float32).astype(
        jnp.bfloat16
    )
    head_shape = (window_count, cell_count, head_count, head_size)
    query_rows = projected[:, :inner_width].reshape(head_shape)
    key_vectors = projected[:, inner_width : 2 * inner_width].reshape(head_shape)
    value_rows = projected[:, 2 * inner_width :].reshape(head_shape)
    scores = (
        jnp.einsum("wmhd,wnhd->whmn", query_rows, key_vectors, preferred_element_type=jnp.float32)
        * score_scale
        + bias_full[None]
    )
    same_region = labels[:, None, :, None] == labels[:, None, None, :]
    scores = jnp.where(same_region, scores, -1e30)
    row_peak = jnp.max(scores, axis=-1, keepdims=True)
    exp_scores = jnp.exp(scores - row_peak)
    attention_weights = exp_scores / jnp.sum(exp_scores, axis=-1, keepdims=True)
    reduced_probability = attention_weights.astype(jnp.bfloat16)
    attended = jnp.einsum(
        "whmn,wnhd->wmhd", reduced_probability, value_rows, preferred_element_type=jnp.float32
    ).astype(jnp.bfloat16)
    stored_residuals = (
        standardized_rows,
        inverse_deviation,
        query_rows,
        key_vectors,
        value_rows,
        attention_weights,
        reduced_probability,
    )
    return (stored_residuals, attended.reshape(-1, inner_width))


def attend_backward(stored_residuals, d_attended, layer_norm_gain, qkv_full):
    (
        standardized_rows,
        inverse_deviation,
        query_rows,
        key_vectors,
        value_rows,
        attention_weights,
        reduced_probability,
    ) = stored_residuals
    head_shape = query_rows.shape
    score_scale = head_shape[3] ** (-0.5)
    total_row_count = standardized_rows.shape[0]
    inner_width = head_shape[2] * head_shape[3]
    d_heads = d_attended.reshape(head_shape)
    d_prob = jnp.einsum("wmhd,wnhd->whmn", d_heads, value_rows, preferred_element_type=jnp.float32)
    d_values = jnp.einsum(
        "whmn,wmhd->wnhd", reduced_probability, d_heads, preferred_element_type=jnp.float32
    ).astype(jnp.bfloat16)
    d_scores = attention_weights * (
        d_prob - jnp.sum(attention_weights * d_prob, axis=-1, keepdims=True)
    )
    table_part = jnp.sum(d_scores, axis=0)
    d_low = d_scores.astype(jnp.bfloat16)
    d_queries = (
        jnp.einsum("whmn,wnhd->wmhd", d_low, key_vectors, preferred_element_type=jnp.float32)
        * score_scale
    ).astype(jnp.bfloat16)
    d_keys = (
        jnp.einsum("whmn,wmhd->wnhd", d_low, query_rows, preferred_element_type=jnp.float32)
        * score_scale
    ).astype(jnp.bfloat16)
    d_projected = jnp.concatenate(
        [
            d_queries.reshape(total_row_count, inner_width),
            d_keys.reshape(total_row_count, inner_width),
            d_values.reshape(total_row_count, inner_width),
        ],
        axis=1,
    )
    normalized_gradient = lax.dot_general(
        d_projected, qkv_full, (((1,), (1,)), ((), ())), preferred_element_type=jnp.float32
    )
    gain_contribution = jnp.sum(normalized_gradient * standardized_rows, axis=0)
    scaled_rows = normalized_gradient * layer_norm_gain
    branch_gradient = inverse_deviation * (
        scaled_rows
        - jnp.mean(scaled_rows, axis=-1, keepdims=True)
        - standardized_rows * jnp.mean(scaled_rows * standardized_rows, axis=-1, keepdims=True)
    )
    return (branch_gradient.astype(jnp.bfloat16), gain_contribution, table_part)


MESH = pl.DeviceIdType.MESH
VMEM = pltpu.VMEM


def on_device(
    sizes,
    pixels,
    cotangent,
    embed_weight,
    embed_bias,
    layer_norm_gain,
    qkv_weight,
    out_weight,
    bias_table,
    rel_index,
    shifts,
):
    images, rows_dev, cols_dev, features = cotangent.shape
    rows, cols, dps = sizes
    head_count, table_size = bias_table.shape
    pix_block, cot_block = pixels[0], cotangent[0]
    row_shift, col_shift = shifts[0, 0], shifts[0, 1]
    qkv_full, out_full = [
        lax.all_gather(
            lax.all_gather(w, "row", axis=0, tiled=True), ("col", "dp"), axis=1, tiled=True
        )
        for w in (qkv_weight, out_weight)
    ]
    pix_r, cot_r = from_behind((pix_block, cot_block), "row", -1)
    pix_c, cot_c = from_behind((pix_block, cot_block[:, :WIN]), "col", -1)
    pix_x, cot_x = from_behind((pix_c, cot_c), "row", -1)
    wide_pix = jnp.concatenate(
        [
            jnp.concatenate([pix_block, pix_c[:, :, : WIN * PATCH]], axis=2),
            jnp.concatenate([pix_r, pix_x[:, :, : WIN * PATCH]], axis=2),
        ],
        axis=1,
    )
    wide_cot = jnp.concatenate(
        [
            jnp.concatenate([cot_block, cot_c], axis=1),
            jnp.concatenate([cot_r, cot_x], axis=1),
        ],
        axis=0,
    )
    wide_patches = make_patches(wide_pix[None])[0]
    patches = lax.dynamic_slice(
        wide_patches, (row_shift, col_shift, 0), (rows_dev, cols_dev, wide_patches.shape[2])
    )
    shifted_cot = lax.dynamic_slice(
        wide_cot, (row_shift, col_shift, 0), (rows_dev, cols_dev, features)
    )
    patch_rows = window_split(patches).reshape(-1, patches.shape[2])
    cot_flat = window_split(shifted_cot).reshape(-1, features)
    grid_rows, grid_cols = rows_dev * rows, cols_dev * cols
    row_ids = lax.axis_index("row") * rows_dev + jnp.arange(rows_dev, dtype=jnp.int32)
    col_ids = lax.axis_index("col") * cols_dev + jnp.arange(cols_dev, dtype=jnp.int32)
    row_part = (row_ids >= grid_rows - row_shift).astype(jnp.int32)
    col_part = (col_ids >= grid_cols - col_shift).astype(jnp.int32)
    region = 2 * row_part[:, None] + col_part[None, :]
    labels = window_split(region[:, :, None])[:, :, 0]
    selector = (
        rel_index.reshape(-1)[:, None] == jnp.arange(table_size, dtype=jnp.int32)[None, :]
    ).astype(jnp.float32)
    bias_full = jnp.dot(selector, bias_table.T, precision=lax.Precision.HIGHEST).T.reshape(
        head_count, WIN * WIN, WIN * WIN
    )
    cells = embed_cells(patch_rows, embed_weight, embed_bias)
    stored_residuals, attended = attend_forward(
        cells.reshape(-1, WIN * WIN, features), labels, layer_norm_gain, qkv_full, bias_full
    )
    d_attended = lax.dot_general(
        cot_flat, out_full, (((1,), (1,)), ((), ())), preferred_element_type=jnp.float32
    ).astype(jnp.bfloat16)
    d_rows, gain_contribution, table_part = attend_backward(
        stored_residuals, d_attended, layer_norm_gain, qkv_full
    )
    table_grad = jnp.dot(
        table_part.reshape(head_count, -1), selector, precision=lax.Precision.HIGHEST
    )
    contract = (((0,), (0,)), ((), ()))
    back_rows = jnp.concatenate([cot_flat, d_rows], axis=0)
    embed_grad = lax.dot_general(
        jnp.concatenate([patch_rows, patch_rows], axis=0),
        back_rows,
        contract,
        preferred_element_type=jnp.float32,
    )
    bias_grad = jnp.sum(back_rows, axis=0, dtype=jnp.float32)
    partial_rows = lax.psum_scatter(
        lax.dot_general(attended, cot_flat, contract, preferred_element_type=jnp.float32),
        "row",
        scatter_dimension=0,
        tiled=True,
    )
    out_weight_grad = lax.psum_scatter(
        partial_rows, ("col", "dp"), scatter_dimension=1, tiled=True
    )
    totals = lax.psum(
        (embed_grad, bias_grad, gain_contribution, table_grad), ("row", "col", "dp")
    )
    return (out_weight_grad,) + totals


def whole_kernel(
    sizes, heads, patch_width,
    shift_ref, qkv_ref, out_ref, cot_o, pat_o, emb_ref, embb_ref, gain_ref, bias_ref, rel_ref,
    grad_out, embed_out, bias_out, gain_out, table_out,
    qkv_all, out_all, cot_c, cot_r, cot_x, pat_c, pat_r, pat_x,
    pat_s, cot_s, xhat_s, inv_s, norm_s, proj_s, datt_s, att_s, dproj_s, bias_s, dtab_s, dn_s,
    gb, core_g, st, a1, b1, t2a, t2b, a2, b2, keep, zs, zr,
    small_s, core_e, es, er, fin,
    send_sem, recv_sem, own_sem, halo_send, halo_recv, red_send, red_recv,
    sml_send, sml_recv, all_send, all_recv, fwd_send, fwd_recv,
):
    bf16, f32, i32 = jnp.bfloat16, jnp.float32, jnp.int32
    rows, cols, dps = sizes
    row, col, dp = lax.axis_index("row"), lax.axis_index("col"), lax.axis_index("dp")
    x, z = row % 2, row // 2
    ring = rows // 2
    top = ring - 1
    core = (col + 1) % 2
    yes = row >= 0
    rows_dev, cols_dev, features = cot_o.shape
    edge = cot_c.shape[1]
    cells = WIN * WIN
    windows = cols_dev // WIN
    inner = att_s.shape[1]
    width = qkv_all.shape[3]
    groups = qkv_all.shape[0]
    out_width = out_all.shape[3]
    scale = (inner // heads) ** -0.5
    sr, sc = shift_ref[0, 0], shift_ref[0, 1]
    span = 2 * cells
    contract_last = (((1,), (1,)), ((), ()))
    contract_first = (((0,), (0,)), ((), ()))

    over_x = {"row": z * 2 + (x + 1) % 2}
    over_y = {"dp": (dp + 1) % 2}
    over_core = {"col": core}
    above_z = {"row": ((z + 1) % ring) * 2 + x}
    below_z = {"row": ((z + top) % ring) * 2 + x}

    def remote(source, target, send, recv, device):
        return pltpu.make_async_remote_copy(
            src_ref=source, dst_ref=target, send_sem=send, recv_sem=recv,
            device_id=device, device_id_type=MESH,
        )

    def flat(ref):
        return ref[...].reshape(-1, ref.shape[-1])

    barrier = pltpu.get_barrier_semaphore()
    others = 0
    for r in range(rows):
        for c in range(cols):
            for d in range(dps):
                if r or c or d:
                    others += 1
                    pl.semaphore_signal(
                        barrier, inc=1,
                        device_id={"row": (row + r) % rows, "col": (col + c) % cols, "dp": (dp + d) % dps},
                        device_id_type=MESH,
                    )
    for pair in range(heads // 2):
        one, two = bias_ref[2 * pair], bias_ref[2 * pair + 1]
        bias_s[pair] = jnp.concatenate([one, one, two, two], axis=1)
    pl.semaphore_wait(barrier, others)

    gathered, own = (qkv_all, out_all), (qkv_ref, out_ref)
    started = []

    def slot(a, flag, dy, dx, k):
        return gathered[a].at[((col + flag) % 2) * 2 + (dp + dy) % 2, k * 2 + (x + dx) % 2]

    def mark(a, flag, dy, dx, k):
        return recv_sem.at[a, ((flag * 2 + dy) * 2 + dx) * ring + k]

    def ship(a, dy, dx, k, device, landing, when, mine=False):
        target = slot(a, 0, dy, dx, k)
        copy = remote(
            own[a] if mine else target, target, send_sem.at[len(started)],
            mark(a, *landing, k), device,
        )
        started.append((copy, when))
        pl.when(when)(copy.start)

    def arrive(a, flag, dy, dx, k, when=yes):
        place = slot(a, flag, dy, dx, k)
        copy = remote(place, place, send_sem.at[0], mark(a, flag, dy, dx, k), over_core)
        pl.when(when)(copy.wait_recv)

    def to_core(a, dy, dx, k, when=yes, mine=False):
        ship(a, dy, dx, k, over_core, (1, dy, dx), when, mine)

    def own_line(a, k, when, up, down, mine=False):
        if up is not None:
            ship(a, 0, 0, k, above_z, (0, 0, 0), when & up, mine)
        if down is not None:
            ship(a, 0, 0, k, below_z, (0, 0, 0), when & down, mine)
        ship(a, 0, 0, k, over_y, (0, 1, 0), when, mine)
        ship(a, 0, 0, k, over_x, (0, 0, 1), when, mine)
        to_core(a, 0, 0, k, when, mine)

    can_up, can_down = z < top, z > 0
    near = z + 1 - 2 * (z % 2)
    low_half = z < ring // 2
    far = (jnp.where(low_half, 2, 1), jnp.where(low_half, 3, 0))

    def clamp(k):
        return jnp.minimum(jnp.maximum(k, 0), top)

    def line_step(a, j):
        below, over = z >= j, z + j <= top
        for k, ok, up, down in (
            (clamp(z - j), below, can_up, None), (clamp(z + j), over, None, can_down)
        ):
            arrive(a, 0, 0, 0, k, ok)
            own_line(a, k, ok, up if j < top else None, down if j < top else None)

    def x_near(a, k):
        arrive(a, 0, 0, 1, k)
        ship(a, 0, 1, k, over_y, (0, 1, 1), yes)
        to_core(a, 0, 1, k)

    def plain(a, dy, dx, k):
        arrive(a, 0, dy, dx, k)
        to_core(a, dy, dx, k)

    def diag_near(a, k):
        arrive(a, 0, 1, 1, k)
        ship(a, 1, 1, k, above_z, (0, 1, 1), z == 1)
        ship(a, 1, 1, k, below_z, (0, 1, 1), z == 2)
        to_core(a, 1, 1, k)

    def diag_far(a, k):
        arrive(a, 0, 1, 1, k)
        ship(a, 1, 1, k, above_z, (0, 1, 1), z == 2)
        ship(a, 1, 1, k, below_z, (0, 1, 1), z == 1)
        to_core(a, 1, 1, k)

    local = [
        pltpu.make_async_copy(own[a], slot(a, 0, 0, 0, z), own_sem.at[a]) for a in range(2)
    ]

    def stage0(a):
        own_line(a, z, yes, can_up, can_down, mine=True)
        local[a].start()

    def stage1(a):
        x_near(a, z)
        line_step(a, 1)
        plain(a, 1, 0, z)

    def stage2(a):
        diag_near(a, z)
        line_step(a, 2)
        x_near(a, near)
        plain(a, 1, 0, near)

    def stage3(a):
        line_step(a, 3)
        diag_near(a, near)
        for k in far:
            plain(a, 0, 1, k)
            plain(a, 1, 0, k)
            diag_far(a, k)

    def stage4(a):
        for dy in range(2):
            for dx in range(2):
                for k in range(ring):
                    arrive(a, 1, dy, dx, k)

    above, left = (row + rows - 1) % rows, (col + cols - 1) % cols
    short = rows_dev - 1
    halos = []

    def halo(source, target, device):
        copy = remote(source, target, halo_send.at[len(halos)], halo_recv.at[len(halos)], device)
        halos.append(copy)
        return copy

    pat_halos = [
        halo(pat_o.at[pl.ds(0, short)], pat_r, {"row": above}),
        halo(pat_o.at[pl.ds(0, short), pl.ds(0, edge)], pat_x, {"row": above, "col": left}),
        halo(pat_o.at[:, pl.ds(0, edge)], pat_c, {"col": left}),
    ]
    cot_side = halo(cot_o.at[:, pl.ds(0, edge)], cot_c, {"col": left})
    cot_down = halo(cot_o.at[pl.ds(0, short)], cot_r, {"row": above})
    cot_corner = halo(cot_r.at[:, pl.ds(0, edge)], cot_x, {"col": left})

    def picks_of(w):
        m = lax.broadcasted_iota(i32, (cells, 1), 0)
        r = (m // WIN) + sr
        c = w * WIN + (m % WIN) + sc
        up, before = r < rows_dev, c < cols_dev
        picks = []
        for ok, high_of, width_of, r_of, c_of in (
            (up & before, rows_dev, cols_dev, 0, 0),
            (up & ~before, rows_dev, edge, 0, cols_dev),
            (~up & before, short, cols_dev, rows_dev, 0),
            (~up & ~before, short, edge, rows_dev, cols_dev),
        ):
            place = jnp.where(ok, (r - r_of) * width_of + (c - c_of), -1)
            lanes = lax.broadcasted_iota(i32, (cells, high_of * width_of), 1)
            picks.append(jnp.where(lanes == place, 1.0, 0.0).astype(bf16))
        return picks

    def pick(picks, parts):
        got = None
        for one, ref in zip(picks, parts):
            term = jnp.dot(one, flat(ref), preferred_element_type=f32)
            got = term if got is None else got + term
        return got.astype(bf16)

    def prologue(w, carry):
        at = pl.ds(pl.multiple_of(w * cells, cells), cells)
        patch = pick(picks_of(w), (pat_o, pat_c, pat_r, pat_x))
        pat_s[at] = patch
        token = (
            jnp.dot(patch, emb_ref[...], preferred_element_type=f32) + embb_ref[...]
        ).astype(bf16).astype(f32)
        mean = jnp.mean(token, axis=-1, keepdims=True)
        centered = token - mean
        inv = lax.rsqrt(jnp.mean(centered * centered, axis=-1, keepdims=True) + norm_epsilon)
        xhat = centered * inv
        xhat_s[at] = xhat
        inv_s[at] = jnp.broadcast_to(inv, (cells, 128))
        norm_s[at] = (xhat * gain_ref[...]).astype(bf16)
        return carry

    def pick_cot(w, carry):
        at = pl.ds(pl.multiple_of(w * cells, cells), cells)
        cot_s[at] = pick(picks_of(w), (cot_o, cot_c, cot_r, cot_x))
        return carry

    def project():
        for g in range(groups):
            proj_s[:, g * width : (g + 1) * width] = jnp.dot(
                norm_s[...], flat(qkv_all.at[g]), preferred_element_type=f32
            ).astype(bf16)

    def attended_cot():
        datt = None
        for g in range(groups):
            term = lax.dot_general(
                cot_s[:, g * out_width : (g + 1) * out_width], flat(out_all.at[g]),
                contract_last, preferred_element_type=f32,
            )
            datt = term if datt is None else datt + term
        datt_s[...] = datt.astype(bf16)

    def mask_of(wp):
        m = lax.broadcasted_iota(i32, (span, 1), 0)
        n = lax.broadcasted_iota(i32, (1, 2 * span), 1) % span

        def label(cell):
            win = cell // cells
            r = row * rows_dev + (cell % cells) // WIN
            c = col * cols_dev + (wp * 2 + win) * WIN + cell % WIN
            down = (r >= rows * rows_dev - sr).astype(i32)
            over = (c >= cols * cols_dev - sc).astype(i32)
            return win * 4 + down * 2 + over

        return label(m) == label(n)

    masks = [mask_of(wp) for wp in range(windows // 2)]
    first = lax.broadcasted_iota(i32, (span, span), 1) < cells
    zero = jnp.zeros((span, span), bf16)

    def attend(hp, carry):
        at = pl.multiple_of(hp * span, span)
        bias = bias_s[hp]
        bias = jnp.concatenate([bias, bias], axis=0)
        kept = None
        for wp in range(windows // 2):
            rs = slice(wp * span, (wp + 1) * span)
            q = proj_s[rs, pl.ds(at, span)]
            k = proj_s[rs, pl.ds(inner + at, span)]
            v = proj_s[rs, pl.ds(2 * inner + at, span)]
            do = datt_s[rs, pl.ds(at, span)]
            ks = jnp.concatenate([jnp.where(first, k, zero), jnp.where(first, zero, k)], axis=0)
            vs = jnp.concatenate([jnp.where(first, v, zero), jnp.where(first, zero, v)], axis=0)
            s = lax.dot_general(q, ks, contract_last, preferred_element_type=f32)
            s = jnp.where(masks[wp], s * scale + bias, -1e30)
            dprob = lax.dot_general(do, vs, contract_last, preferred_element_type=f32)
            ps, dss = [], []
            for half in range(2):
                part = s[:, half * span : (half + 1) * span]
                e = jnp.exp(part - jnp.max(part, axis=-1, keepdims=True))
                p = e * (1.0 / jnp.sum(e, axis=-1, keepdims=True))
                d = dprob[:, half * span : (half + 1) * span]
                dss.append(p * (d - jnp.sum(p * d, axis=-1, keepdims=True)))
                ps.append(p)
            p_low = jnp.concatenate(ps, axis=1).astype(bf16)
            ds = jnp.concatenate(dss, axis=1)
            d_low = ds.astype(bf16)
            tab = ds[:cells] + ds[cells:]
            kept = tab if kept is None else kept + tab
            att_s[rs, pl.ds(at, span)] = jnp.dot(p_low, vs, preferred_element_type=f32).astype(bf16)
            dv = lax.dot_general(p_low, do, contract_first, preferred_element_type=f32)
            dq = jnp.dot(d_low, ks, preferred_element_type=f32) * scale
            dk = lax.dot_general(d_low, q, contract_first, preferred_element_type=f32) * scale
            dproj_s[rs, pl.ds(at, span)] = dq.astype(bf16)
            dproj_s[rs, pl.ds(inner + at, span)] = jnp.where(first, dk[:span], dk[span:]).astype(bf16)
            dproj_s[rs, pl.ds(2 * inner + at, span)] = jnp.where(first, dv[:span], dv[span:]).astype(bf16)
        dtab_s[hp] = kept
        return carry

    def back_project():
        for g in range(groups):
            term = lax.dot_general(
                dproj_s[:, g * width : (g + 1) * width], flat(qkv_all.at[g]),
                contract_last, preferred_element_type=f32,
            )
            if g == 0:
                dn_s[...] = term
            else:
                dn_s[...] += term

    def finish(w, gain_sum):
        at = pl.ds(pl.multiple_of(w * cells, cells), cells)
        dn = dn_s[at]
        xhat = xhat_s[at]
        gain_sum = gain_sum + jnp.sum(dn * xhat, axis=0, keepdims=True)
        g_rows = dn * gain_ref[...]
        mean = jnp.mean(g_rows, axis=-1, keepdims=True)
        along = jnp.mean(g_rows * xhat, axis=-1, keepdims=True)
        norm_s[at] = (inv_s[at][:, :1] * (g_rows - mean - xhat * along)).astype(bf16)
        return gain_sum

    entries = lax.broadcasted_iota(i32, (256, 2 * span), 0)

    def table_step(i, carry):
        for u in range(4):
            at = i * 4 + u
            spread = jnp.where(entries == rel_ref[pl.ds(at, 1), :], 1.0, 0.0).astype(bf16)
            one, two = dtab_s[:, at * 2, :], dtab_s[:, at * 2 + 1, :]
            part = jnp.concatenate(
                [
                    jnp.concatenate([one[:, :span], two[:, :span]], axis=1),
                    jnp.concatenate([one[:, span:], two[:, span:]], axis=1),
                ],
                axis=0,
            )
            high = part.astype(bf16).astype(f32)
            both = jnp.concatenate([high, part - high], axis=0).astype(bf16)
            carry = carry + lax.dot_general(both, spread, contract_last, preferred_element_type=f32)
        return carry

    pending = []

    def swap(index, source, target, device):
        copy = remote(source, target, red_send.at[index], red_recv.at[index], device)
        copy.start()
        pending.append(copy)
        return copy

    def grad_make():
        for g in range(groups):
            block = lax.dot_general(
                att_s[...], cot_s[:, g * out_width : (g + 1) * out_width],
                contract_first, preferred_element_type=f32,
            )
            gb[g] = block.astype(bf16).reshape(gb.shape[1:])
        return swap(0, gb.at[pl.ds(core * 2, 2)], core_g, over_core)

    half_rows = st.shape[4]

    def grad_first(got):
        got.wait_recv()
        for d in range(2):
            for r in range(rows):
                total = (gb[col * 2 + d, r].astype(f32) + core_g[d, r].astype(f32)).astype(bf16)
                st[0, d, r % 2, r // 2] = total[:half_rows]
                st[1, d, r % 2, r // 2] = total[half_rows:]
        return (
            swap(1, st.at[0, (dp + 1) % 2], a1, over_y),
            swap(2, st.at[1, :, (x + 1) % 2], b1, over_x),
        )

    def grad_second(got):
        for copy in got:
            copy.wait_recv()
        away, other = (x + 1) % 2, (dp + 1) % 2
        t2a[...] = (st[0, dp, away].astype(f32) + a1[away].astype(f32)).astype(bf16)
        t2b[...] = (st[1, other, x].astype(f32) + b1[other].astype(f32)).astype(bf16)
        sent = (swap(3, t2a, a2, over_x), swap(4, t2b, b2, over_y))
        keep[0] = st[0, dp, x].astype(f32) + a1[x].astype(f32)
        keep[1] = st[1, dp, x].astype(f32) + b1[dp].astype(f32)
        return sent

    def grad_third(got):
        for copy in got:
            copy.wait_recv()
        keep[0] += a2[...].astype(f32)
        keep[1] += b2[...].astype(f32)
        sent = []
        for s in range(1, ring):
            for h in range(2):
                zs[s, h] = keep[h, (z + s) % ring].astype(bf16)
            sent.append(swap(4 + s, zs.at[s], zr.at[s], {"row": ((z + s) % ring) * 2 + x}))
        return sent

    def grad_last(got):
        for copy in got:
            copy.wait_recv()
        for h in range(2):
            total = keep[h, z]
            for s in range(1, ring):
                total = total + zr[s, h].astype(f32)
            grad_out[h * half_rows : (h + 1) * half_rows] = total

    for copy in pat_halos:
        copy.start()
    stage0(0)
    cot_side.start()
    stage1(0)
    for copy in pat_halos:
        copy.wait_recv()
    lax.fori_loop(0, windows, prologue, 0)
    stage2(0)
    stage0(1)
    stage3(0)
    cot_down.start()
    stage1(1)
    stage4(0)
    local[0].wait()
    project()
    stage2(1)
    stage3(1)
    cot_down.wait_recv()
    cot_corner.start()
    stage4(1)
    local[1].wait()
    cot_side.wait_recv()
    cot_corner.wait_recv()
    lax.fori_loop(0, windows, pick_cot, 0)
    attended_cot()
    lax.fori_loop(0, heads // 2, attend, 0)
    got = grad_make()
    back_project()
    got = grad_first(got)
    tab = lax.fori_loop(0, cells // 8, table_step, jnp.zeros((2 * heads, 256), f32))
    tab = tab[:heads] + tab[heads:]
    got = grad_second(got)
    gain_sum = lax.fori_loop(0, windows, finish, jnp.zeros((1, features), f32))
    patch = pat_s[...]
    embed = lax.dot_general(patch, cot_s[...], contract_first, preferred_element_type=f32)
    embed = embed + lax.dot_general(patch, norm_s[...], contract_first, preferred_element_type=f32)
    depth = embed.shape[0]
    wide = features // cols
    for c in range(cols):
        for rg in range(depth // 8):
            for lh in range(wide // 256):
                at = c * wide + lh * 256
                small_s[c, rg * (wide // 256) + lh] = embed[rg * 8 : rg * 8 + 8, at : at + 256]
    per = wide // 256
    base = patch_width // 8
    for c in range(cols):
        for lh in range(per):
            at = c * wide + lh * 256
            small_s[c, base * per + lh, 1:2] = gain_sum[:, at : at + 256]
    small_s[0, base * per, 2:8] = tab[: heads // 2]
    small_s[0, (base + 1) * per, 0 : heads // 2] = tab[heads // 2 :]
    flip = remote(small_s.at[core], core_e, sml_send.at[0], sml_recv.at[0], over_core)
    flip.start()
    got = grad_third(got)
    flip.wait_recv()
    es[...] = small_s[col] + core_e[...]
    spread = []
    for r in range(rows):
        for d in range(dps):
            if r or d:
                to_row, to_dp = (row + r) % rows, (dp + d) % dps
                index = r * dps + d
                copy = remote(
                    es.at[to_row * dps + to_dp], er.at[index], sml_send.at[index], sml_recv.at[index],
                    {"row": to_row, "dp": to_dp},
                )
                copy.start()
                spread.append(copy)
    mine = row * dps + dp
    for copy in spread:
        copy.wait_recv()
    whole = es[mine]
    for index in range(1, rows * dps):
        whole = whole + er[index]
    fin[col, mine] = whole
    tell = []
    hand = remote(fin.at[col, mine], fin.at[col, mine], fwd_send.at[0], fwd_recv.at[0], over_core)
    for r in range(rows):
        for d in range(dps):
            if r or d:
                index = r * dps + d
                copy = remote(
                    fin.at[col, mine], fin.at[col, mine], all_send.at[index], all_recv.at[index],
                    {"row": (row + r) % rows, "dp": (dp + d) % dps},
                )
                copy.start()
                tell.append(copy)
    hand.start()
    grad_last(got)
    for r in range(rows):
        for d in range(dps):
            if r or d:
                index = r * dps + d
                part = ((row + rows - r) % rows) * dps + (dp + dps - d) % dps
                place = fin.at[col, part]
                remote(place, place, all_send.at[index], all_recv.at[index], over_core).wait_recv()
                copy = remote(place, place, fwd_send.at[index], fwd_recv.at[index], over_core)
                copy.start()
                tell.append(copy)
    for r in range(rows):
        for d in range(dps):
            index = r * dps + d
            part = ((row + rows - r) % rows) * dps + (dp + dps - d) % dps
            place = fin.at[core, part]
            remote(place, place, fwd_send.at[index], fwd_recv.at[index], over_core).wait_recv()
    for c in range(cols):
        for lh in range(per):
            at = c * wide + lh * 256
            for rg in range(base):
                embed_out[rg * 8 : rg * 8 + 8, at : at + 256] = fin[c, rg * per + lh]
            bias_out[:, at : at + 256] = fin[c, base * per + lh, 0:1]
            gain_out[:, at : at + 256] = fin[c, base * per + lh, 1:2]
    for i in range(heads // 2):
        table_out[2 * i : 2 * i + 1] = fin[0, base * per, 2 + i : 3 + i]
        table_out[2 * i + 1 : 2 * i + 2] = fin[0, (base + 1) * per, i : i + 1]
    for copy, when in started:
        pl.when(when)(copy.wait_send)
    for copy in halos + pending + [flip] + spread + tell + [hand]:
        copy.wait_send()


def direct_device(
    sizes, pixels, cotangent, embed_weight, embed_bias, layer_norm_gain,
    qkv_weight, out_weight, bias_table, rel_index, shifts,
):
    rows, cols, dps = sizes
    ring = rows // 2
    heads, table_size = bias_table.shape
    patch_width, features = embed_weight.shape
    bf16, f32 = jnp.bfloat16, jnp.float32
    cot_block = cotangent[0]
    rows_dev, cols_dev, _ = cot_block.shape
    groups = cols * dps
    depth = 64
    cells = WIN * WIN
    patches = make_patches(pixels)[0]
    tail = jnp.zeros(patches.shape[:2] + (depth - patch_width,), bf16).at[:, :, 0].set(1)
    pat_block = jnp.concatenate([patches, tail], axis=2)
    selector = (
        rel_index.reshape(-1)[:, None] == jnp.arange(table_size, dtype=jnp.int32)[None, :]
    ).astype(f32)
    bias_full = jnp.dot(selector, bias_table.T, precision=lax.Precision.HIGHEST).T.reshape(
        heads, cells, cells
    )
    twice = jnp.concatenate([rel_index, rel_index], axis=1).reshape(cells // 2, 4 * cells)
    inner = out_weight.shape[0] * rows
    here = rows_dev * cols_dev
    big = out_weight.shape
    half = big[0] // 2
    dma = pltpu.SemaphoreType.DMA
    vmem = pl.BlockSpec(memory_space=VMEM)
    sums = (rows * dps, 8, 256)
    grad, embed, bias, gain, table = pl.pallas_call(
        functools.partial(whole_kernel, sizes, heads, patch_width),
        out_shape=[
            jax.ShapeDtypeStruct(big, f32),
            jax.ShapeDtypeStruct((patch_width, features), f32),
            jax.ShapeDtypeStruct((1, features), f32),
            jax.ShapeDtypeStruct((1, features), f32),
            jax.ShapeDtypeStruct((heads, 256), f32),
        ],
        in_specs=[pl.BlockSpec(memory_space=pltpu.SMEM)] + [vmem] * 9,
        out_specs=[vmem] * 5,
        scratch_shapes=[
            VMEM((groups, rows) + qkv_weight.shape, bf16),
            VMEM((groups, rows) + big, bf16),
            VMEM((rows_dev, WIN, features), bf16),
            VMEM((rows_dev - 1, cols_dev, features), bf16),
            VMEM((rows_dev - 1, WIN, features), bf16),
            VMEM((rows_dev, WIN, depth), bf16),
            VMEM((rows_dev - 1, cols_dev, depth), bf16),
            VMEM((rows_dev - 1, WIN, depth), bf16),
            VMEM((here, depth), bf16),
            VMEM((here, features), bf16),
            VMEM((here, features), f32),
            VMEM((here, 128), f32),
            VMEM((here, features), bf16),
            VMEM((here, 3 * inner), bf16),
            VMEM((here, inner), bf16),
            VMEM((here, inner), bf16),
            VMEM((here, 3 * inner), bf16),
            VMEM((heads // 2, cells, 4 * cells), f32),
            VMEM((heads // 2, cells, 4 * cells), f32),
            VMEM((here, features), f32),
            VMEM((groups, rows) + big, bf16),
            VMEM((2, rows) + big, bf16),
            VMEM((2, 2, 2, ring, half, big[1]), bf16),
            VMEM((2, ring, half, big[1]), bf16),
            VMEM((2, ring, half, big[1]), bf16),
            VMEM((ring, half, big[1]), bf16),
            VMEM((ring, half, big[1]), bf16),
            VMEM((ring, half, big[1]), bf16),
            VMEM((ring, half, big[1]), bf16),
            VMEM((2, ring, half, big[1]), f32),
            VMEM((ring, 2, half, big[1]), bf16),
            VMEM((ring, 2, half, big[1]), bf16),
            VMEM((cols,) + sums, f32),
            VMEM(sums, f32), VMEM(sums, f32), VMEM(sums, f32),
            VMEM((cols,) + sums, f32),
            dma((200,)), dma((2, 8 * ring)), dma((2,)), dma((6,)), dma((6,)),
            dma((8,)), dma((8,)),
            dma((rows * dps,)), dma((rows * dps,)), dma((rows * dps,)), dma((rows * dps,)),
            dma((rows * dps,)), dma((rows * dps,)),
        ],
        compiler_params=pltpu.CompilerParams(
            collective_id=0, has_side_effects=True, vmem_limit_bytes=60 * 2**20
        ),
        name="whole",
    )(
        shifts, qkv_weight, out_weight, cot_block, pat_block,
        jnp.pad(embed_weight, ((0, depth - patch_width), (0, 0))),
        embed_bias[None], layer_norm_gain[None], bias_full, twice,
    )
    return (grad, embed, bias[0], gain[0], table[:, :table_size])


def solution(mesh):
    sizes = tuple(mesh.shape[name] for name in ("row", "col", "dp"))
    direct = sizes[1:] == (2, 2) and sizes[0] == 8
    return jax.shard_map(
        functools.partial(direct_device if direct else on_device, sizes),
        mesh=mesh,
        in_specs=(
            P("dp", None, "row", "col"),
            P("dp", "row", "col", None),
            P(),
            P(),
            P(),
            P("row", ("col", "dp")),
            P("row", ("col", "dp")),
            P(),
            P(),
            P("dp", None),
        ),
        out_specs=(P("row", ("col", "dp")), P(), P(), P(), P()),
        check_vma=False,
    )
```

time: 204 us -> 120 us (0.59)
  local copies, waits for them, and re-layouts: 43.5 us -> 13.4 us
  matrix products: 25.7 us -> 2.58 us
  Pallas kernels: 120 us -> 103 us
  other arithmetic: 6.65 us -> 0.8 us
  between operations: 6.44 us -> 0.69 us
    dot_general x17 -> x1, matrix products: 25.7 us -> 2.58 us  [direct_device(): jnp.dot(selector, bias_table.T, precision=lax.Precision.HIGHEST)]
    pallas_call x2 -> x1, Pallas kernels: 120 us -> 103 us  [direct_device(): pl.pallas_call(functools.partial(whole_kernel, sizes, heads, patch_width)...]
    reshape x16 -> x3, local copies, waits for them, and re-layouts: 12.2 us -> 3.98 us  [the longest x1 2.45 us: make_patches(): pixel_block.reshape(images, channels, grid_rows, PATCH, grid_cols, PATCH)]
    concatenate x1 -> x0, local copies, waits for them, and re-layouts: 8.12 us -> none  [on_device(): jnp.concatenate([w.reshape(-1, qkv_weight.shape[1]) for w in qkv_all], ax...]
    another operation x5 -> x1, local copies, waits for them, and re-layouts: 7.13 us -> 0.14 us  [direct_device(): patches = make_patches(pixels)[0]]
    slice x6 -> x0, local copies, waits for them, and re-layouts: 3.8 us -> none  [the longest x1 1.79 us: on_device(): cot_groups[:, k]]
    convert_element_type x4 -> x0, local copies, waits for them, and re-layouts: 2.68 us -> none  [the longest x1 0.85 us: attend_backward(): d_keys = (jnp.einsum('whmn,wmhd->wnhd', d_low, query_rows, preferred_elem...]
    sub x1 -> x0, other arithmetic: 2.35 us -> none  [attend_forward(): exp_scores = jnp.exp(scores - row_peak)]
where the time goes in v1:
time: 120 us
  Pallas kernels  103 us (86%)
  local copies, waits for them, and re-layouts  13.4 us (11%)
  matrix products  2.58 us (2%)
    pallas_call x1, Pallas kernels, direct_device(): pl.pallas_call(functools.partial(whole_kernel, sizes, heads, patch_width)...  103 us
    unnamed x16, local copies, waits for them, and re-layouts  7.85 us
    dot_general x1, matrix products, direct_device(): jnp.dot(selector, bias_table.T, precision=lax.Precision.HIGHEST)  2.58 us
    reshape x1, local copies, waits for them, and re-layouts, make_patches(): pixel_block.reshape(images, channels, grid_rows, PATCH, grid_cols, PATCH)  2.45 us

profile of v1, /device:TPU:1, one launch (start us, length us, event | category | flops | bytes accessed | tf_op | source)
XLA Modules:
  0.0 120.0 jit_solution(11731626147183690918)
XLA Ops:
  0.6 0.0 copy-start
  0.6 0.0 copy-start.4
  0.7 2.4 %reshape.48 = bf16[1,3,8,4,32,4]{5,4,3,2,1,0:T(8,128)(2,1)S(1)} reshape(bf16[1,3,32,128]{3,2,1,0:T(8,128)(2,1)} %param.12) | data formatting | bytes 49152 | tf_op jit(solution)/shard_map/reshape | solution.py:27
  3.1 0.0 copy-start.2
  3.1 0.7 copy.17
  3.8 0.1 copy.18
  3.9 0.0 copy-done.4
  3.9 0.7 pad_maximum_fusion.pat_o
  4.7 0.0 copy-done.2
  4.7 0.1 eq.15
  4.7 0.0 copy-done
  4.7 0.0 copy-start.1
  4.7 0.0 copy-start.3
  4.8 2.6 %convolution_bitcast_fusion = f32[12,4096]{1,0:T(8,128)S(1)} fusion(f32[12,225]{1,0:T(8,128)S(1)} %copy-done, s32[4096]{0:T(1024)S(1)} %eq.15), kind=kOutput, calls=%fused_computation | convolution fusion | flops 133632000 | bytes 223792 | tf_op jit(solution)/shard_map/dot_general | solution.py:806
  7.3 0.9 reshape.49.bias_ref
  8.2 0.0 copy-done.1
  8.3 0.8 copy.19.qkv_ref
  9.1 0.0 copy-done.3
  9.1 0.7 pad.6.emb_ref
  9.7 0.1 pad_add_fusion
  9.8 0.6 reshape.50.rel_ref
  10.4 102.6 %whole.1 = (f32[96,256]{1,0:T(8,128)}, f32[48,1024]{1,0:T(8,128)}, f32[1,1024]{1,0:T(1,128)}, f32[1,1024]{1,0:T(1,128)}, f32[12,256]{1,0:T(8,128)}) custom-call(s32[1,2]{1,0:T(1,128)} %shift_ref.1, bf16[128,576]{1,0:T(8,128)(2,1)} %copy.19.qkv_ref, bf16[96,256]{1,0:T(8,128)(2,1)} %out_ref.1, bf16[8,32,1024]{2,1,0:T(8,128)(2,1)} %bitcast.14, ...), custom_call_target="tpu_custom_call" | custom-call | tf_op jit(solution)/shard_map/whole/pallas_call | solution.py:817
  113.0 1.5 %copy.25 = f32[96,256]{1,0:T(8,128)} copy(f32[96,256]{1,0:T(8,128)} %get-tuple-element.32) | data formatting | bytes 196608
  114.6 1.6 %copy.26 = f32[48,1024]{1,0:T(8,128)} copy(f32[48,1024]{1,0:T(8,128)} %get-tuple-element.33) | data formatting | bytes 393216
  116.2 1.3 %copy.27 = f32[1024]{0:T(1024)} copy(f32[1024]{0:T(1024)} %bitcast.20) | data formatting | bytes 8192
  117.4 1.3 %copy.28 = f32[1024]{0:T(1024)} copy(f32[1024]{0:T(1024)} %bitcast.19) | data formatting | bytes 8192
  118.7 1.3 %copy.29 = f32[12,225]{1,0:T(8,128)} copy(f32[12,225]{1,0:T(8,128)} %bitcast.16) | data formatting | bytes 21600
Async XLA Ops:
  0.6 4.1 %copy-start = (f32[12,225]{1,0:T(8,128)S(1)}, f32[12,225]{1,0:T(8,128)}, u32[]{:S(2)}) copy-start(f32[12,225]{1,0:T(8,128)} %param.19) | copy-start | bytes 32404
  0.6 3.3 %copy-start.4 = (bf16[8,32,16]{2,1,0:T(8,128)(2,1)S(1)}, bf16[8,32,16]{2,1,0:T(8,128)(2,1)}, u32[]{:S(2)}) copy-start(bf16[8,32,16]{2,1,0:T(8,128)(2,1)} %constant.31.clone.1) | copy-start | bytes 24580
  3.1 1.6 %copy-start.2 = (s32[64,64]{1,0:T(8,128)S(1)}, s32[64,64]{1,0:T(8,128)}, u32[]{:S(2)}) copy-start(s32[64,64]{1,0:T(8,128)} %param.20) | copy-start | bytes 49156
  4.7 3.5 %copy-start.1 = (bf16[128,576]{0,1:T(8,128)(2,1)S(1)}, bf16[128,576]{0,1:T(8,128)(2,1)}, u32[]{:S(2)}) copy-start(bf16[128,576]{0,1:T(8,128)(2,1)} %param.17) | copy-start | bytes 442372
  4.7 4.3 %copy-start.3 = (bf16[48,1024]{1,0:T(8,128)(2,1)S(1)}, bf16[48,1024]{1,0:T(8,128)(2,1)}, u32[]{:S(2)}) copy-start(bf16[48,1024]{1,0:T(8,128)(2,1)} %param.14) | copy-start | bytes 294916

commit v2 on v1

--- a/solution.py
+++ b/solution.py
@@ -251,11 +251,14 @@
     return (out_weight_grad,) + totals
 
 
+UNROLL = 6
+
+
 def whole_kernel(
     sizes, heads, patch_width,
-    shift_ref, qkv_ref, out_ref, cot_o, pat_o, emb_ref, embb_ref, gain_ref, bias_ref, rel_ref,
+    shift_ref, qkv_ref, out_ref, cot_ref, pix_ref, emb_ref, embb_ref, gain_ref, tab_ref, rel_ref,
     grad_out, embed_out, bias_out, gain_out, table_out,
-    qkv_all, out_all, cot_c, cot_r, cot_x, pat_c, pat_r, pat_x,
+    qkv_all, out_all, cot_o, pat_o, rel_s, bias_t, p_s, cot_c, cot_r, cot_x, pat_c, pat_r, pat_x,
     pat_s, cot_s, xhat_s, inv_s, norm_s, proj_s, datt_s, att_s, dproj_s, bias_s, dtab_s, dn_s,
     gb, core_g, st, a1, b1, t2a, t2b, a2, b2, keep, zs, zr,
     small_s, core_e, es, er, fin,
@@ -275,7 +278,7 @@
     cells = WIN * WIN
     windows = cols_dev // WIN
     inner = att_s.shape[1]
-    width = qkv_all.shape[3]
+    chip_rows = qkv_all.shape[3]
     groups = qkv_all.shape[0]
     out_width = out_all.shape[3]
     scale = (inner // heads) ** -0.5
@@ -311,115 +314,132 @@
                         device_id={"row": (row + r) % rows, "col": (col + c) % cols, "dp": (dp + d) % dps},
                         device_id_type=MESH,
                     )
-    for pair in range(heads // 2):
-        one, two = bias_ref[2 * pair], bias_ref[2 * pair + 1]
-        bias_s[pair] = jnp.concatenate([one, one, two, two], axis=1)
+    local = [
+        pltpu.make_async_copy(source, target, own_sem.at[i])
+        for i, (source, target) in enumerate(
+            (
+                (qkv_ref, qkv_all.at[col * 2 + dp, row]),
+                (out_ref, out_all.at[col * 2 + dp, row]),
+                (cot_ref.at[0], cot_o),
+            )
+        )
+    ]
+    for copy in local:
+        copy.start()
     pl.semaphore_wait(barrier, others)
 
-    gathered, own = (qkv_all, out_all), (qkv_ref, out_ref)
+    def patchify():
+        depth = pat_o.shape[2]
+        channels, pixel_rows, pixel_cols = pix_ref.shape[1:]
+        pix = pix_ref[0].reshape(channels * pixel_rows, pixel_cols)
+        area = PATCH * PATCH
+        f = lax.broadcasted_iota(i32, (depth, 1), 0)
+        source_row = jnp.where(f < patch_width, (f // area) * pixel_rows + (f % area) // PATCH, -1024)
+        row_lane = lax.broadcasted_iota(i32, (depth, channels * pixel_rows), 1)
+        column = lax.broadcasted_iota(i32, (depth, pixel_cols), 1) % PATCH
+        spot = lax.broadcasted_iota(i32, (cols_dev, pixel_cols), 1) // PATCH
+        join = jnp.where(spot == lax.broadcasted_iota(i32, (cols_dev, pixel_cols), 0), 1.0, 0.0).astype(bf16)
+        last = lax.broadcasted_iota(i32, (cols_dev, depth), 1) == patch_width
+        for i in range(rows_dev):
+            choose = jnp.where(row_lane == source_row + i * PATCH, 1.0, 0.0).astype(bf16)
+            wide = jnp.dot(choose, pix, preferred_element_type=f32)
+            wide = jnp.where(column == f % PATCH, wide, 0.0).astype(bf16)
+            cell = lax.dot_general(join, wide, contract_last, preferred_element_type=f32)
+            pat_o[i] = jnp.where(last, 1.0, cell).astype(bf16)
+        rel_s[...] = jnp.concatenate([rel_ref[...], rel_ref[...]], axis=1)
+
     started = []
+    parts = 2
+    step = qkv_all.shape[2] // parts
+    last_a = parts
 
     def slot(a, flag, dy, dx, k):
-        return gathered[a].at[((col + flag) % 2) * 2 + (dp + dy) % 2, k * 2 + (x + dx) % 2]
+        which = ((col + flag) % 2) * 2 + (dp + dy) % 2, k * 2 + (x + dx) % 2
+        if a == last_a:
+            return out_all.at[which]
+        return qkv_all.at[which[0], which[1], pl.ds(a * step, step)]
 
     def mark(a, flag, dy, dx, k):
         return recv_sem.at[a, ((flag * 2 + dy) * 2 + dx) * ring + k]
 
-    def ship(a, dy, dx, k, device, landing, when, mine=False):
+    def ship(a, dy, dx, k, device, landing, when):
         target = slot(a, 0, dy, dx, k)
-        copy = remote(
-            own[a] if mine else target, target, send_sem.at[len(started)],
-            mark(a, *landing, k), device,
-        )
+        copy = remote(target, target, send_sem.at[len(started)], mark(a, *landing, k), device)
         started.append((copy, when))
         pl.when(when)(copy.start)
 
-    def arrive(a, flag, dy, dx, k, when=yes):
+    def arrive(a, flag, dy, dx, k, when):
         place = slot(a, flag, dy, dx, k)
         copy = remote(place, place, send_sem.at[0], mark(a, flag, dy, dx, k), over_core)
         pl.when(when)(copy.wait_recv)
 
-    def to_core(a, dy, dx, k, when=yes, mine=False):
-        ship(a, dy, dx, k, over_core, (1, dy, dx), when, mine)
-
-    def own_line(a, k, when, up, down, mine=False):
-        if up is not None:
-            ship(a, 0, 0, k, above_z, (0, 0, 0), when & up, mine)
-        if down is not None:
-            ship(a, 0, 0, k, below_z, (0, 0, 0), when & down, mine)
-        ship(a, 0, 0, k, over_y, (0, 1, 0), when, mine)
-        ship(a, 0, 0, k, over_x, (0, 0, 1), when, mine)
-        to_core(a, 0, 0, k, when, mine)
-
     can_up, can_down = z < top, z > 0
-    near = z + 1 - 2 * (z % 2)
-    low_half = z < ring // 2
-    far = (jnp.where(low_half, 2, 1), jnp.where(low_half, 3, 0))
+    middle = (z == 1) | (z == 2)
 
     def clamp(k):
         return jnp.minimum(jnp.maximum(k, 0), top)
 
-    def line_step(a, j):
-        below, over = z >= j, z + j <= top
-        for k, ok, up, down in (
-            (clamp(z - j), below, can_up, None), (clamp(z + j), over, None, can_down)
-        ):
-            arrive(a, 0, 0, 0, k, ok)
-            own_line(a, k, ok, up if j < top else None, down if j < top else None)
-
-    def x_near(a, k):
-        arrive(a, 0, 0, 1, k)
-        ship(a, 0, 1, k, over_y, (0, 1, 1), yes)
-        to_core(a, 0, 1, k)
-
-    def plain(a, dy, dx, k):
-        arrive(a, 0, dy, dx, k)
-        to_core(a, dy, dx, k)
-
-    def diag_near(a, k):
-        arrive(a, 0, 1, 1, k)
-        ship(a, 1, 1, k, above_z, (0, 1, 1), z == 1)
-        ship(a, 1, 1, k, below_z, (0, 1, 1), z == 2)
-        to_core(a, 1, 1, k)
-
-    def diag_far(a, k):
-        arrive(a, 0, 1, 1, k)
-        ship(a, 1, 1, k, above_z, (0, 1, 1), z == 2)
-        ship(a, 1, 1, k, below_z, (0, 1, 1), z == 1)
-        to_core(a, 1, 1, k)
-
-    local = [
-        pltpu.make_async_copy(own[a], slot(a, 0, 0, 0, z), own_sem.at[a]) for a in range(2)
-    ]
-
-    def stage0(a):
-        own_line(a, z, yes, can_up, can_down, mine=True)
-        local[a].start()
-
-    def stage1(a):
-        x_near(a, z)
-        line_step(a, 1)
-        plain(a, 1, 0, z)
-
-    def stage2(a):
-        diag_near(a, z)
-        line_step(a, 2)
-        x_near(a, near)
-        plain(a, 1, 0, near)
-
-    def stage3(a):
-        line_step(a, 3)
-        diag_near(a, near)
-        for k in far:
-            plain(a, 0, 1, k)
-            plain(a, 1, 0, k)
-            diag_far(a, k)
-
-    def stage4(a):
+    def around(j):
+        if j == 0:
+            return ((z, yes, 0),)
+        return ((clamp(z - j), z >= j, 1), (clamp(z + j), z + j <= top, -1))
+
+    def spread_own(a, k, when, way, j):
+        if way >= 0 and j < top:
+            ship(a, 0, 0, k, above_z, (0, 0, 0), when & can_up)
+        if way <= 0 and j < top:
+            ship(a, 0, 0, k, below_z, (0, 0, 0), when & can_down)
+        ship(a, 0, 0, k, over_y, (0, 1, 0), when)
+        ship(a, 0, 0, k, over_x, (0, 0, 1), when)
+        ship(a, 0, 0, k, over_core, (1, 0, 0), when)
+
+    def line(a, j):
+        for k, when, way in around(j):
+            arrive(a, 0, 0, 0, k, when)
+            spread_own(a, k, when, way, j)
+
+    def x_line(a, j):
+        for k, when, _ in around(j):
+            arrive(a, 0, 0, 1, k, when)
+            if a == last_a:
+                ship(a, 0, 1, k, over_y, (0, 1, 1), when)
+            elif j == 0:
+                ship(a, 0, 1, k, over_y, (0, 1, 1), when)
+            ship(a, 0, 1, k, over_core, (1, 0, 1), when)
+
+    def y_line(a, j):
+        for k, when, _ in around(j):
+            arrive(a, 0, 1, 0, k, when)
+            if a != last_a and j == 1:
+                ship(a, 1, 0, k, over_x, (0, 1, 1), when & (k // 2 == z // 2))
+            ship(a, 1, 0, k, over_core, (1, 1, 0), when)
+
+    def diagonal(a, j):
+        for k, when, _ in around(j):
+            arrive(a, 0, 1, 1, k, when)
+            if a != last_a and j < 3:
+                ship(a, 1, 1, k, above_z, (0, 1, 1), when & middle & (k < 2))
+                ship(a, 1, 1, k, below_z, (0, 1, 1), when & middle & (k >= 2))
+            ship(a, 1, 1, k, over_core, (1, 1, 1), when)
+
+    def hop(a, h):
+        if h == 0:
+            spread_own(a, z, yes, 0, 0)
+            return
+        if h < ring:
+            line(a, h)
+        if h <= ring:
+            x_line(a, h - 1)
+        if 2 <= h <= ring + 1:
+            diagonal(a, h - 2)
+        if h <= ring:
+            y_line(a, h - 1)
+
+    def partner(a):
         for dy in range(2):
             for dx in range(2):
                 for k in range(ring):
-                    arrive(a, 1, dy, dx, k)
+                    arrive(a, 1, dy, dx, k, yes)
 
     above, left = (row + rows - 1) % rows, (col + cols - 1) % cols
     short = rows_dev - 1
@@ -436,7 +456,10 @@
         halo(pat_o.at[:, pl.ds(0, edge)], pat_c, {"col": left}),
     ]
     cot_side = halo(cot_o.at[:, pl.ds(0, edge)], cot_c, {"col": left})
-    cot_down = halo(cot_o.at[pl.ds(0, short)], cot_r, {"row": above})
+    cuts = [(r, min(2, short - r)) for r in range(0, short, 2)]
+    cot_down = [
+        halo(cot_o.at[pl.ds(r, n)], cot_r.at[pl.ds(r, n)], {"row": above}) for r, n in cuts
+    ]
     cot_corner = halo(cot_r.at[:, pl.ds(0, edge)], cot_x, {"col": left})
 
     def picks_of(w):
@@ -468,7 +491,7 @@
         patch = pick(picks_of(w), (pat_o, pat_c, pat_r, pat_x))
         pat_s[at] = patch
         token = (
-            jnp.dot(patch, emb_ref[...], preferred_element_type=f32) + embb_ref[...]
+            jnp.dot(patch[:, :patch_width], emb_ref[...], preferred_element_type=f32) + embb_ref[...]
         ).astype(bf16).astype(f32)
         mean = jnp.mean(token, axis=-1, keepdims=True)
         centered = token - mean
@@ -484,10 +507,14 @@
         cot_s[at] = pick(picks_of(w), (cot_o, cot_c, cot_r, cot_x))
         return carry
 
+    def weight_rows(r):
+        return jnp.concatenate([qkv_all[g, r] for g in range(groups)], axis=0)
+
     def project():
-        for g in range(groups):
-            proj_s[:, g * width : (g + 1) * width] = jnp.dot(
-                norm_s[...], flat(qkv_all.at[g]), preferred_element_type=f32
+        full = jnp.concatenate([weight_rows(r) for r in range(rows)], axis=1)
+        for n in range(0, 3 * inner, inner):
+            proj_s[:, n : n + inner] = lax.dot_general(
+                norm_s[...], full[n : n + inner], contract_last, preferred_element_type=f32
             ).astype(bf16)
 
     def attended_cot():
@@ -518,36 +545,53 @@
     first = lax.broadcasted_iota(i32, (span, span), 1) < cells
     zero = jnp.zeros((span, span), bf16)
 
+    def stacked(value):
+        return jnp.concatenate([jnp.where(first, value, zero), jnp.where(first, zero, value)], axis=0)
+
     def attend(hp, carry):
         at = pl.multiple_of(hp * span, span)
         bias = bias_s[hp]
         bias = jnp.concatenate([bias, bias], axis=0)
+        for wp in range(windows // 2):
+            rs = slice(wp * span, (wp + 1) * span)
+            q = proj_s[rs, pl.ds(at, span)]
+            ks = stacked(proj_s[rs, pl.ds(inner + at, span)])
+            vs = stacked(proj_s[rs, pl.ds(2 * inner + at, span)])
+            s = lax.dot_general(q, ks, contract_last, preferred_element_type=f32)
+            s = jnp.where(masks[wp], s * scale + bias, -1e30)
+            ps = []
+            for half in range(2):
+                part = s[:, half * span : (half + 1) * span]
+                e = jnp.exp(part - jnp.max(part, axis=-1, keepdims=True))
+                ps.append(e * (1.0 / jnp.sum(e, axis=-1, keepdims=True)))
+            p = jnp.concatenate(ps, axis=1)
+            p_s[hp, wp] = p
+            att_s[rs, pl.ds(at, span)] = jnp.dot(
+                p.astype(bf16), vs, preferred_element_type=f32
+            ).astype(bf16)
+        return carry
+
+    def attend_back(hp, carry):
+        at = pl.multiple_of(hp * span, span)
         kept = None
         for wp in range(windows // 2):
             rs = slice(wp * span, (wp + 1) * span)
             q = proj_s[rs, pl.ds(at, span)]
-            k = proj_s[rs, pl.ds(inner + at, span)]
-            v = proj_s[rs, pl.ds(2 * inner + at, span)]
+            ks = stacked(proj_s[rs, pl.ds(inner + at, span)])
+            vs = stacked(proj_s[rs, pl.ds(2 * inner + at, span)])
             do = datt_s[rs, pl.ds(at, span)]
-            ks = jnp.concatenate([jnp.where(first, k, zero), jnp.where(first, zero, k)], axis=0)
-            vs = jnp.concatenate([jnp.where(first, v, zero), jnp.where(first, zero, v)], axis=0)
-            s = lax.dot_general(q, ks, contract_last, preferred_element_type=f32)
-            s = jnp.where(masks[wp], s * scale + bias, -1e30)
             dprob = lax.dot_general(do, vs, contract_last, preferred_element_type=f32)
-            ps, dss = [], []
+            p = p_s[hp, wp]
+            dss = []
             for half in range(2):
-                part = s[:, half * span : (half + 1) * span]
-                e = jnp.exp(part - jnp.max(part, axis=-1, keepdims=True))
-                p = e * (1.0 / jnp.sum(e, axis=-1, keepdims=True))
+                part = p[:, half * span : (half + 1) * span]
                 d = dprob[:, half * span : (half + 1) * span]
-                dss.append(p * (d - jnp.sum(p * d, axis=-1, keepdims=True)))
-                ps.append(p)
-            p_low = jnp.concatenate(ps, axis=1).astype(bf16)
+                dss.append(part * (d - jnp.sum(part * d, axis=-1, keepdims=True)))
+            p_low = p.astype(bf16)
             ds = jnp.concatenate(dss, axis=1)
             d_low = ds.astype(bf16)
             tab = ds[:cells] + ds[cells:]
             kept = tab if kept is None else kept + tab
-            att_s[rs, pl.ds(at, span)] = jnp.dot(p_low, vs, preferred_element_type=f32).astype(bf16)
             dv = lax.dot_general(p_low, do, contract_first, preferred_element_type=f32)
             dq = jnp.dot(d_low, ks, preferred_element_type=f32) * scale
             dk = lax.dot_general(d_low, q, contract_first, preferred_element_type=f32) * scale
@@ -558,15 +602,11 @@
         return carry
 
     def back_project():
-        for g in range(groups):
-            term = lax.dot_general(
-                dproj_s[:, g * width : (g + 1) * width], flat(qkv_all.at[g]),
-                contract_last, preferred_element_type=f32,
+        for r in range(0, rows, 2):
+            two = jnp.concatenate([weight_rows(r), weight_rows(r + 1)], axis=1)
+            dn_s[:, r * chip_rows : (r + 2) * chip_rows] = jnp.dot(
+                dproj_s[...], two, preferred_element_type=f32
             )
-            if g == 0:
-                dn_s[...] = term
-            else:
-                dn_s[...] += term
 
     def finish(w, gain_sum):
         at = pl.ds(pl.multiple_of(w * cells, cells), cells)
@@ -581,10 +621,42 @@
 
     entries = lax.broadcasted_iota(i32, (256, 2 * span), 0)
 
+    def spread_of(at):
+        pair = jnp.concatenate([rel_s[pl.ds(2 * at, 1), :], rel_s[pl.ds(2 * at + 1, 1), :]], axis=1)
+        return jnp.where(entries == pair, 1.0, 0.0).astype(bf16)
+
+    def bias_make(start, stop, final):
+        order = [tab_ref[i : i + 1, :] for i in list(range(0, heads, 2)) + list(range(1, heads, 2))]
+        rest = jnp.concatenate(order, axis=0)
+        rest = jnp.concatenate(
+            [rest, jnp.zeros((heads, 256 - rest.shape[1]), f32)], axis=1
+        )
+        terms = []
+        for _ in range(3):
+            low = rest.astype(bf16)
+            terms.append(low)
+            rest = rest - low.astype(f32)
+        stack = jnp.concatenate([t.astype(f32) for t in terms], axis=0).astype(bf16)
+
+        def one(i, carry):
+            for u in range(4):
+                at = i * 4 + u
+                got = jnp.dot(stack, spread_of(at), preferred_element_type=f32)
+                got = got[:heads] + got[heads : 2 * heads] + got[2 * heads :]
+                for v in range(2):
+                    piece = got[:, v * span : (v + 1) * span]
+                    m = 2 * at + v
+                    bias_t[m, : heads // 2, :span] = piece[: heads // 2]
+                    bias_t[m, : heads // 2, span:] = piece[heads // 2 :]
+            return carry
+
+        lax.fori_loop(start, stop, one, 0)
+        for pair in range(heads // 2 if final else 0):
+            bias_s[pair] = bias_t[:, pair, :]
+
     def table_step(i, carry):
         for u in range(4):
             at = i * 4 + u
-            spread = jnp.where(entries == rel_ref[pl.ds(at, 1), :], 1.0, 0.0).astype(bf16)
             one, two = dtab_s[:, at * 2, :], dtab_s[:, at * 2 + 1, :]
             part = jnp.concatenate(
                 [
@@ -595,7 +667,9 @@
             )
             high = part.astype(bf16).astype(f32)
             both = jnp.concatenate([high, part - high], axis=0).astype(bf16)
-            carry = carry + lax.dot_general(both, spread, contract_last, preferred_element_type=f32)
+            carry = carry + lax.dot_general(
+                both, spread_of(at), contract_last, preferred_element_type=f32
+            )
         return carry
 
     pending = []
@@ -661,39 +735,63 @@
                 total = total + zr[s, h].astype(f32)
             grad_out[h * half_rows : (h + 1) * half_rows] = total
 
+    def unrolled(body):
+        def several(i, carry):
+            for u in range(UNROLL):
+                body(i * UNROLL + u, carry)
+            return carry
+
+        lax.fori_loop(0, heads // 2 // UNROLL, several, 0)
+
+    local[0].wait()
+    local[1].wait()
+    every = parts + 1
+
+    def hops(h):
+        for a in range(every):
+            hop(a, h)
+
+    hops(0)
+    patchify()
     for copy in pat_halos:
         copy.start()
-    stage0(0)
+    local[2].wait()
     cot_side.start()
-    stage1(0)
+    cot_down[0].start()
+    hops(1)
+    bias_make(0, cells // 16, False)
+    for copy in cot_down[1:-1]:
+        copy.start()
+    hops(2)
     for copy in pat_halos:
         copy.wait_recv()
-    lax.fori_loop(0, windows, prologue, 0)
-    stage2(0)
-    stage0(1)
-    stage3(0)
-    cot_down.start()
-    stage1(1)
-    stage4(0)
-    local[0].wait()
-    project()
-    stage2(1)
-    stage3(1)
-    cot_down.wait_recv()
+    lax.fori_loop(0, windows // 2, prologue, 0)
+    cot_down[-1].start()
+    hops(3)
+    lax.fori_loop(windows // 2, windows, prologue, 0)
+    hops(4)
+    bias_make(cells // 16, cells // 8, True)
+    for copy in cot_down:
+        copy.wait_recv()
     cot_corner.start()
-    stage4(1)
-    local[1].wait()
+    hops(5)
     cot_side.wait_recv()
     cot_corner.wait_recv()
     lax.fori_loop(0, windows, pick_cot, 0)
+    for a in range(parts):
+        partner(a)
+    project()
+    unrolled(attend)
+    got = grad_make()
+    partner(last_a)
     attended_cot()
-    lax.fori_loop(0, heads // 2, attend, 0)
-    got = grad_make()
-    back_project()
     got = grad_first(got)
+    unrolled(attend_back)
+    got = grad_second(got)
     tab = lax.fori_loop(0, cells // 8, table_step, jnp.zeros((2 * heads, 256), f32))
     tab = tab[:heads] + tab[heads:]
-    got = grad_second(got)
+    back_project()
+    got = grad_third(got)
     gain_sum = lax.fori_loop(0, windows, finish, jnp.zeros((1, features), f32))
     patch = pat_s[...]
     embed = lax.dot_general(patch, cot_s[...], contract_first, preferred_element_type=f32)
@@ -715,7 +813,6 @@
     small_s[0, (base + 1) * per, 0 : heads // 2] = tab[heads // 2 :]
     flip = remote(small_s.at[core], core_e, sml_send.at[0], sml_recv.at[0], over_core)
     flip.start()
-    got = grad_third(got)
     flip.wait_recv()
     es[...] = small_s[col] + core_e[...]
     spread = []
@@ -792,21 +889,10 @@
     heads, table_size = bias_table.shape
     patch_width, features = embed_weight.shape
     bf16, f32 = jnp.bfloat16, jnp.float32
-    cot_block = cotangent[0]
-    rows_dev, cols_dev, _ = cot_block.shape
+    _, rows_dev, cols_dev, _ = cotangent.shape
     groups = cols * dps
     depth = 64
     cells = WIN * WIN
-    patches = make_patches(pixels)[0]
-    tail = jnp.zeros(patches.shape[:2] + (depth - patch_width,), bf16).at[:, :, 0].set(1)
-    pat_block = jnp.concatenate([patches, tail], axis=2)
-    selector = (
-        rel_index.reshape(-1)[:, None] == jnp.arange(table_size, dtype=jnp.int32)[None, :]
-    ).astype(f32)
-    bias_full = jnp.dot(selector, bias_table.T, precision=lax.Precision.HIGHEST).T.reshape(
-        heads, cells, cells
-    )
-    twice = jnp.concatenate([rel_index, rel_index], axis=1).reshape(cells // 2, 4 * cells)
     inner = out_weight.shape[0] * rows
     here = rows_dev * cols_dev
     big = out_weight.shape
@@ -823,11 +909,16 @@
             jax.ShapeDtypeStruct((1, features), f32),
             jax.ShapeDtypeStruct((heads, 256), f32),
         ],
-        in_specs=[pl.BlockSpec(memory_space=pltpu.SMEM)] + [vmem] * 9,
+        in_specs=[pl.BlockSpec(memory_space=pltpu.SMEM)] + [pl.BlockSpec(memory_space=pl.ANY)] * 3 + [vmem] * 6,
         out_specs=[vmem] * 5,
         scratch_shapes=[
-            VMEM((groups, rows) + qkv_weight.shape, bf16),
+            VMEM((groups, rows) + qkv_weight.shape[::-1], bf16),
             VMEM((groups, rows) + big, bf16),
+            VMEM((rows_dev, cols_dev, features), bf16),
+            VMEM((rows_dev, cols_dev, depth), bf16),
+            VMEM((cells, 2 * cells), jnp.int32),
+            VMEM((cells, 8 * pl.cdiv(heads, 16), 4 * cells), f32),
+            VMEM((heads // 2, cols_dev // (2 * WIN), 2 * cells, 4 * cells), f32),
             VMEM((rows_dev, WIN, features), bf16),
             VMEM((rows_dev - 1, cols_dev, features), bf16),
             VMEM((rows_dev - 1, WIN, features), bf16),
@@ -861,7 +952,7 @@
             VMEM((cols,) + sums, f32),
             VMEM(sums, f32), VMEM(sums, f32), VMEM(sums, f32),
             VMEM((cols,) + sums, f32),
-            dma((200,)), dma((2, 8 * ring)), dma((2,)), dma((6,)), dma((6,)),
+            dma((400,)), dma((3, 8 * ring)), dma((3,)), dma((16,)), dma((16,)),
             dma((8,)), dma((8,)),
             dma((rows * dps,)), dma((rows * dps,)), dma((rows * dps,)), dma((rows * dps,)),
             dma((rows * dps,)), dma((rows * dps,)),
@@ -871,9 +962,8 @@
         ),
         name="whole",
     )(
-        shifts, qkv_weight, out_weight, cot_block, pat_block,
-        jnp.pad(embed_weight, ((0, depth - patch_width), (0, 0))),
-        embed_bias[None], layer_norm_gain[None], bias_full, twice,
+        shifts, qkv_weight.T, out_weight, cotangent, pixels, embed_weight,
+        embed_bias[None], layer_norm_gain[None], bias_table, rel_index,
     )
     return (grad, embed, bias[0], gain[0], table[:, :table_size])
 

time: 120 us -> 90.4 us (0.75)
  Pallas kernels: 103 us -> 85.3 us
  local copies, waits for them, and re-layouts: 13.4 us -> 4.14 us
  matrix products: 2.58 us -> 0 us
    pallas_call x1, Pallas kernels: 103 us -> 85.3 us  [direct_device(): pl.pallas_call(functools.partial(whole_kernel, sizes, heads, patch_width)...]
    reshape x3 -> x0, local copies, waits for them, and re-layouts: 3.98 us -> none  [the longest x1 2.45 us: make_patches(): pixel_block.reshape(images, channels, grid_rows, PATCH, grid_cols, PATCH)]
    unnamed x16 -> x13, local copies, waits for them, and re-layouts: 7.85 us -> 4.14 us
    dot_general x1 -> x0, matrix products: 2.58 us -> none  [direct_device(): jnp.dot(selector, bias_table.T, precision=lax.Precision.HIGHEST)]
where the time goes in v2:
time: 90.4 us; the launch traced here: 90.1 us
  Pallas kernels  85.3 us (94%)
  local copies, waits for them, and re-layouts  4.14 us (5%)
    pallas_call x1, Pallas kernels, direct_device(): pl.pallas_call(functools.partial(whole_kernel, sizes, heads, patch_width)...  85.3 us
    unnamed x13, local copies, waits for them, and re-layouts  4.14 us

profile of v2, /device:TPU:1, one launch (start us, length us, event | category | flops | bytes accessed | tf_op | source)
XLA Modules:
  0.0 90.1 jit_solution(16077351503188878142)
XLA Ops:
  0.6 85.3 %whole.1 = (f32[96,256]{1,0:T(8,128)}, f32[48,1024]{1,0:T(8,128)}, f32[1,1024]{1,0:T(1,128)}, f32[1,1024]{1,0:T(1,128)}, f32[12,256]{1,0:T(8,128)}) custom-call(s32[1,2]{1,0:T(1,128)} %shift_ref.1, bf16[576,128]{1,0:T(8,128)(2,1)} %bitcast.6, bf16[96,256]{1,0:T(8,128)(2,1)} %out_ref.1, bf16[1,8,32,1024]{3,2,1,0:T(8,128)(2,1)} %cot_ref.1, ...), custom_call_target="tpu_custom_call" | custom-call | tf_op jit(solution)/shard_map/whole/pallas_call | solution.py:903
  86.0 0.0 copy-start
  86.0 1.6 %copy.20 = f32[96,256]{1,0:T(8,128)} copy(f32[96,256]{1,0:T(8,128)} %get-tuple-element.20) | data formatting | bytes 196608
  87.6 0.0 copy-done
  87.6 0.0 copy-start.3
  87.6 0.0 copy-start.1
  87.6 0.7 copy.21
  88.3 0.0 copy-done.3
  88.3 0.0 copy-start.2
  88.3 0.6 copy.22
  88.9 0.1 copy-done.2
  88.9 0.6 copy.23
  89.5 0.0 copy-done.1
  89.5 0.6 copy.24
Async XLA Ops:
  86.0 1.6 %copy-start = (f32[48,1024]{1,0:T(8,128)S(1)}, f32[48,1024]{1,0:T(8,128)}, u32[]{:S(2)}) copy-start(f32[48,1024]{1,0:T(8,128)} %get-tuple-element.21) | copy-start | bytes 589828
  87.6 0.7 copy-start.3
  87.6 1.9 %copy-start.1 = (f32[12,256]{1,0:T(8,128)S(1)}, f32[12,256]{1,0:T(8,128)}, u32[]{:S(2)}) copy-start(f32[12,256]{1,0:T(8,128)} %get-tuple-element.14) | copy-start | bytes 36868
  88.3 0.7 copy-start.2

commit v3 on v2

--- a/solution.py
+++ b/solution.py
@@ -254,6 +254,18 @@
 UNROLL = 6
 
 
+def hand_out(*refs):
+    sems = refs[-1]
+    count = (len(refs) - 1) // 2
+    copies = [
+        pltpu.make_async_copy(refs[i], refs[count + i], sems.at[i]) for i in range(count)
+    ]
+    for copy in copies:
+        copy.start()
+    for copy in copies:
+        copy.wait()
+
+
 def whole_kernel(
     sizes, heads, patch_width,
     shift_ref, qkv_ref, out_ref, cot_ref, pix_ref, emb_ref, embb_ref, gain_ref, tab_ref, rel_ref,
@@ -680,50 +692,63 @@
         pending.append(copy)
         return copy
 
+    away, over = (x + 1) % 2, (dp + 1) % 2
+
+    def grad_block(g):
+        at = pl.ds(pl.multiple_of(g * out_width, out_width), out_width)
+        block = lax.dot_general(
+            att_s[...], cot_s[:, at], contract_first, preferred_element_type=f32
+        )
+        gb[g] = block.astype(bf16).reshape(gb.shape[1:])
+
     def grad_make():
-        for g in range(groups):
-            block = lax.dot_general(
-                att_s[...], cot_s[:, g * out_width : (g + 1) * out_width],
-                contract_first, preferred_element_type=f32,
-            )
-            gb[g] = block.astype(bf16).reshape(gb.shape[1:])
-        return swap(0, gb.at[pl.ds(core * 2, 2)], core_g, over_core)
+        sent = []
+        for i, d in enumerate((over, dp)):
+            grad_block(core * 2 + d)
+            sent.append(swap(8 + i, gb.at[core * 2 + d], core_g.at[d], over_core))
+        for d in (over, dp):
+            grad_block(col * 2 + d)
+        return sent
 
     half_rows = st.shape[4]
 
     def grad_first(got):
-        got.wait_recv()
-        for d in range(2):
+        sent = []
+        for i, d in enumerate((over, dp)):
+            got[i].wait_recv()
             for r in range(rows):
                 total = (gb[col * 2 + d, r].astype(f32) + core_g[d, r].astype(f32)).astype(bf16)
                 st[0, d, r % 2, r // 2] = total[:half_rows]
                 st[1, d, r % 2, r // 2] = total[half_rows:]
-        return (
-            swap(1, st.at[0, (dp + 1) % 2], a1, over_y),
-            swap(2, st.at[1, :, (x + 1) % 2], b1, over_x),
-        )
+            if i == 0:
+                sent.append(swap(1, st.at[0, over], a1, over_y))
+        sent.append(swap(2, st.at[1, :, away], b1, over_x))
+        return sent
 
     def grad_second(got):
-        for copy in got:
-            copy.wait_recv()
-        away, other = (x + 1) % 2, (dp + 1) % 2
+        got[0].wait_recv()
         t2a[...] = (st[0, dp, away].astype(f32) + a1[away].astype(f32)).astype(bf16)
-        t2b[...] = (st[1, other, x].astype(f32) + b1[other].astype(f32)).astype(bf16)
-        sent = (swap(3, t2a, a2, over_x), swap(4, t2b, b2, over_y))
+        sent = [swap(3, t2a, a2, over_x)]
+        got[1].wait_recv()
+        t2b[...] = (st[1, over, x].astype(f32) + b1[over].astype(f32)).astype(bf16)
+        sent.append(swap(4, t2b, b2, over_y))
         keep[0] = st[0, dp, x].astype(f32) + a1[x].astype(f32)
         keep[1] = st[1, dp, x].astype(f32) + b1[dp].astype(f32)
         return sent
 
     def grad_third(got):
-        for copy in got:
-            copy.wait_recv()
-        keep[0] += a2[...].astype(f32)
-        keep[1] += b2[...].astype(f32)
         sent = []
-        for s in range(1, ring):
-            for h in range(2):
+        for h, ref in enumerate((a2, b2)):
+            got[h].wait_recv()
+            keep[h] += ref[...].astype(f32)
+            for s in range(1, ring):
                 zs[s, h] = keep[h, (z + s) % ring].astype(bf16)
-            sent.append(swap(4 + s, zs.at[s], zr.at[s], {"row": ((z + s) % ring) * 2 + x}))
+                sent.append(
+                    swap(
+                        10 + s * 2 + h, zs.at[s, h], zr.at[s, h],
+                        {"row": ((z + s) % ring) * 2 + x},
+                    )
+                )
         return sent
 
     def grad_last(got):
@@ -787,9 +812,9 @@
     attended_cot()
     got = grad_first(got)
     unrolled(attend_back)
-    got = grad_second(got)
     tab = lax.fori_loop(0, cells // 8, table_step, jnp.zeros((2 * heads, 256), f32))
     tab = tab[:heads] + tab[heads:]
+    got = grad_second(got)
     back_project()
     got = grad_third(got)
     gain_sum = lax.fori_loop(0, windows, finish, jnp.zeros((1, features), f32))
@@ -833,7 +858,7 @@
     whole = es[mine]
     for index in range(1, rows * dps):
         whole = whole + er[index]
-    fin[col, mine] = whole
+    fin[col, mine] = whole.astype(bf16)
     tell = []
     hand = remote(fin.at[col, mine], fin.at[col, mine], fwd_send.at[0], fwd_recv.at[0], over_core)
     for r in range(rows):
@@ -868,12 +893,16 @@
         for lh in range(per):
             at = c * wide + lh * 256
             for rg in range(base):
-                embed_out[rg * 8 : rg * 8 + 8, at : at + 256] = fin[c, rg * per + lh]
-            bias_out[:, at : at + 256] = fin[c, base * per + lh, 0:1]
-            gain_out[:, at : at + 256] = fin[c, base * per + lh, 1:2]
+                embed_out[rg * 8 : rg * 8 + 8, at : at + 256] = fin[c, rg * per + lh].astype(f32)
+            rest = fin[c, base * per + lh].astype(f32)
+            bias_out[:, at : at + 256] = rest[0:1]
+            gain_out[:, at : at + 256] = rest[1:2]
+    entries_out = table_out.shape[1]
+    ones = fin[0, base * per].astype(f32)[:, :entries_out]
+    twos = fin[0, (base + 1) * per].astype(f32)[:, :entries_out]
     for i in range(heads // 2):
-        table_out[2 * i : 2 * i + 1] = fin[0, base * per, 2 + i : 3 + i]
-        table_out[2 * i + 1 : 2 * i + 2] = fin[0, (base + 1) * per, i : i + 1]
+        table_out[2 * i : 2 * i + 1] = ones[2 + i : 3 + i]
+        table_out[2 * i + 1 : 2 * i + 2] = twos[i : i + 1]
     for copy, when in started:
         pl.when(when)(copy.wait_send)
     for copy in halos + pending + [flip] + spread + tell + [hand]:
@@ -907,7 +936,7 @@
             jax.ShapeDtypeStruct((patch_width, features), f32),
             jax.ShapeDtypeStruct((1, features), f32),
             jax.ShapeDtypeStruct((1, features), f32),
-            jax.ShapeDtypeStruct((heads, 256), f32),
+            jax.ShapeDtypeStruct((heads, table_size), f32),
         ],
         in_specs=[pl.BlockSpec(memory_space=pltpu.SMEM)] + [pl.BlockSpec(memory_space=pl.ANY)] * 3 + [vmem] * 6,
         out_specs=[vmem] * 5,
@@ -951,9 +980,9 @@
             VMEM((ring, 2, half, big[1]), bf16),
             VMEM((cols,) + sums, f32),
             VMEM(sums, f32), VMEM(sums, f32), VMEM(sums, f32),
-            VMEM((cols,) + sums, f32),
+            VMEM((cols,) + sums, bf16),
             dma((400,)), dma((3, 8 * ring)), dma((3,)), dma((16,)), dma((16,)),
-            dma((8,)), dma((8,)),
+            dma((20,)), dma((20,)),
             dma((rows * dps,)), dma((rows * dps,)), dma((rows * dps,)), dma((rows * dps,)),
             dma((rows * dps,)), dma((rows * dps,)),
         ],
@@ -965,7 +994,16 @@
         shifts, qkv_weight.T, out_weight, cotangent, pixels, embed_weight,
         embed_bias[None], layer_norm_gain[None], bias_table, rel_index,
     )
-    return (grad, embed, bias[0], gain[0], table[:, :table_size])
+    results = (grad, embed, bias, gain, table)
+    grad, embed, bias, gain, table = pl.pallas_call(
+        hand_out,
+        out_shape=[jax.ShapeDtypeStruct(value.shape, value.dtype) for value in results],
+        in_specs=[vmem] * 5,
+        out_specs=[pl.BlockSpec(memory_space=pl.ANY)] * 5,
+        scratch_shapes=[dma((5,))],
+        name="hand_out",
+    )(*results)
+    return (grad, embed, bias[0], gain[0], table)
 
 
 def solution(mesh):

time: 90.4 us -> 86.7 us (0.959)
  local copies, waits for them, and re-layouts: 4.14 us -> 0 us
    unnamed x13 -> x0, local copies, waits for them, and re-layouts: 4.14 us -> none
    pallas_call x0 -> x1, Pallas kernels: none -> 1.76 us  [direct_device(): pl.pallas_call(hand_out, out_shape=[jax.ShapeDtypeStruct(value.shape, val...]
    pallas_call x1, Pallas kernels: 85.3 us -> 84.2 us  [direct_device(): pl.pallas_call(functools.partial(whole_kernel, sizes, heads, patch_width)...]
where the time goes in v3:
time: 86.7 us; the launch traced here: 86.6 us
  Pallas kernels  85.9 us (99%)
    pallas_call x1, Pallas kernels, direct_device(): pl.pallas_call(functools.partial(whole_kernel, sizes, heads, patch_width)...  84.2 us
    pallas_call x1, Pallas kernels, direct_device(): pl.pallas_call(hand_out, out_shape=[jax.ShapeDtypeStruct(value.shape, val...  1.76 us

profile of v3, /device:TPU:1, one launch (start us, length us, event | category | flops | bytes accessed | tf_op | source)
XLA Modules:
  0.0 86.6 jit_solution(7441744788025642239)
XLA Ops:
  0.6 84.2 %whole.1 = (f32[96,256]{1,0:T(8,128)}, f32[48,1024]{1,0:T(8,128)}, f32[1,1024]{1,0:T(1,128)}, f32[1,1024]{1,0:T(1,128)}, f32[12,225]{1,0:T(8,128)}) custom-call(s32[1,2]{1,0:T(1,128)} %shift_ref.1, bf16[576,128]{1,0:T(8,128)(2,1)} %bitcast.5, bf16[96,256]{1,0:T(8,128)(2,1)} %out_ref.1, bf16[1,8,32,1024]{3,2,1,0:T(8,128)(2,1)} %cot_ref.1, ...), custom_call_target="tpu_custom_call" | custom-call | tf_op jit(solution)/shard_map/whole/pallas_call | solution.py:932
  84.8 1.8 %hand_out.1 = (f32[96,256]{1,0:T(8,128)}, f32[48,1024]{1,0:T(8,128)}, f32[1,1024]{1,0:T(1,128)}, f32[1,1024]{1,0:T(1,128)}, f32[12,225]{1,0:T(8,128)}) custom-call(f32[96,256]{1,0:T(8,128)} %get-tuple-element.15.refs_0_, f32[48,1024]{1,0:T(8,128)} %get-tuple-element.16.refs_1_, f32[1,1024]{1,0:T(1,128)} %get-tuple-element.17.refs_2_, ...), custom_call_target="tpu_custom_call" | custom-call | tf_op jit(solution)/shard_map/hand_out/pallas_call | solution.py:998

commit v4 on v3

--- a/solution.py
+++ b/solution.py
@@ -785,13 +785,12 @@
     cot_down[0].start()
     hops(1)
     bias_make(0, cells // 16, False)
-    for copy in cot_down[1:-1]:
+    for copy in cot_down[1:]:
         copy.start()
     hops(2)
     for copy in pat_halos:
         copy.wait_recv()
     lax.fori_loop(0, windows // 2, prologue, 0)
-    cot_down[-1].start()
     hops(3)
     lax.fori_loop(windows // 2, windows, prologue, 0)
     hops(4)
@@ -839,7 +838,7 @@
     flip = remote(small_s.at[core], core_e, sml_send.at[0], sml_recv.at[0], over_core)
     flip.start()
     flip.wait_recv()
-    es[...] = small_s[col] + core_e[...]
+    es[...] = (small_s[col] + core_e[...]).astype(bf16)
     spread = []
     for r in range(rows):
         for d in range(dps):
@@ -855,9 +854,9 @@
     mine = row * dps + dp
     for copy in spread:
         copy.wait_recv()
-    whole = es[mine]
+    whole = small_s[col, mine] + core_e[mine]
     for index in range(1, rows * dps):
-        whole = whole + er[index]
+        whole = whole + er[index].astype(f32)
     fin[col, mine] = whole.astype(bf16)
     tell = []
     hand = remote(fin.at[col, mine], fin.at[col, mine], fwd_send.at[0], fwd_recv.at[0], over_core)
@@ -979,7 +978,7 @@
             VMEM((ring, 2, half, big[1]), bf16),
             VMEM((ring, 2, half, big[1]), bf16),
             VMEM((cols,) + sums, f32),
-            VMEM(sums, f32), VMEM(sums, f32), VMEM(sums, f32),
+            VMEM(sums, f32), VMEM(sums, bf16), VMEM(sums, bf16),
             VMEM((cols,) + sums, bf16),
             dma((400,)), dma((3, 8 * ring)), dma((3,)), dma((16,)), dma((16,)),
             dma((20,)), dma((20,)),

time: 86.7 us -> 85.7 us (0.988)
  Pallas kernels: 85.9 us -> 84.8 us
    pallas_call x1, Pallas kernels: 84.2 us -> 83.1 us  [direct_device(): pl.pallas_call(functools.partial(whole_kernel, sizes, heads, patch_width)...]
where the time goes in v4:
time: 85.7 us; the launch traced here: 85.5 us
  Pallas kernels  84.8 us (99%)
    pallas_call x1, Pallas kernels, direct_device(): pl.pallas_call(functools.partial(whole_kernel, sizes, heads, patch_width)...  83.1 us
    pallas_call x1, Pallas kernels, direct_device(): pl.pallas_call(hand_out, out_shape=[jax.ShapeDtypeStruct(value.shape, val...  1.76 us

profile of v4, /device:TPU:1, one launch (start us, length us, event | category | flops | bytes accessed | tf_op | source)
XLA Modules:
  0.0 85.5 jit_solution(8751711267405038307)
XLA Ops:
  0.6 83.1 %whole.1 = (f32[96,256]{1,0:T(8,128)}, f32[48,1024]{1,0:T(8,128)}, f32[1,1024]{1,0:T(1,128)}, f32[1,1024]{1,0:T(1,128)}, f32[12,225]{1,0:T(8,128)}) custom-call(s32[1,2]{1,0:T(1,128)} %shift_ref.1, bf16[576,128]{1,0:T(8,128)(2,1)} %bitcast.5, bf16[96,256]{1,0:T(8,128)(2,1)} %out_ref.1, bf16[1,8,32,1024]{3,2,1,0:T(8,128)(2,1)} %cot_ref.1, ...), custom_call_target="tpu_custom_call" | custom-call | tf_op jit(solution)/shard_map/whole/pallas_call | solution.py:931
  83.7 1.8 %hand_out.1 = (f32[96,256]{1,0:T(8,128)}, f32[48,1024]{1,0:T(8,128)}, f32[1,1024]{1,0:T(1,128)}, f32[1,1024]{1,0:T(1,128)}, f32[12,225]{1,0:T(8,128)}) custom-call(f32[96,256]{1,0:T(8,128)} %get-tuple-element.15.refs_0_, f32[48,1024]{1,0:T(8,128)} %get-tuple-element.16.refs_1_, f32[1,1024]{1,0:T(1,128)} %get-tuple-element.17.refs_2_, ...), custom_call_target="tpu_custom_call" | custom-call | tf_op jit(solution)/shard_map/hand_out/pallas_call | solution.py:997
